TPU v7x, 8 devices: a whole 2x2x1 slice. The times are simulated.
8 devices in a mesh: dp: 1 (over z), ep: 2 (over y), tp: 4 (over x, core).
Axes of the slice: x: 2, y: 2, z: 1, core: 2. Of those that a mesh axis runs over, the one named last changes fastest.
Arguments:
- X: bfloat16 [256, 2048], P(('dp', 'ep', 'tp'))
- idx: int32 [256, 8], P(('dp', 'ep', 'tp'))
- g: float32 [256, 8], P(('dp', 'ep', 'tp'))
- W1: bfloat16 [64, 2048, 1024], P('ep', None, 'tp')
- W3: bfloat16 [64, 2048, 1024], P('ep', None, 'tp')
- W2: bfloat16 [64, 1024, 2048], P('ep', 'tp')
Outputs:
- output: bfloat16 [256, 2048], P(('dp', 'ep', 'tp'))
All inputs are finite; a program needn't handle non-finite values.
Results may differ from a plain program's by a relative error of at most 0.0101844.
Values are sent between devices in bfloat16 or wider.
A program may use at most 1 GiB of HBM per device.

v0:
```python
import jax
import jax.numpy as jnp
from jax import lax
from jax.sharding import PartitionSpec as P

CF = 2


def _route(idx, n_exp, cap):
    ids = idx.reshape(-1)
    oh = (ids[:, None] == jnp.arange(n_exp, dtype=jnp.int32)[None, :]).astype(jnp.int32)
    s = jnp.sum(oh * (jnp.cumsum(oh, axis=0) - 1), axis=1)
    keep = s < cap
    return jnp.where(keep, ids * cap + s, n_exp * cap), keep


def solution(mesh):
    ep, tp = mesh.shape["ep"], mesh.shape["tp"]
    rows = P(("dp", "ep", "tp"), None)

    def local(x, idx, g, w1, w3, w2):
        t_loc, d = x.shape
        top = idx.shape[1]
        el = w1.shape[0]
        n_exp = el * ep
        cap = CF * top * t_loc // n_exp
        dest, keep = _route(idx, n_exp, cap)
        xr = jnp.repeat(x, top, axis=0)
        buf = jnp.zeros((n_exp * cap, d), x.dtype).at[dest].set(xr, mode="drop").reshape(ep, el, cap, d)
        recv = lax.all_to_all(buf, "ep", 0, 0, tiled=True)
        allr = lax.all_gather(recv, "tp", axis=0)
        xe = allr.transpose(2, 0, 1, 3, 4).reshape(el, tp * ep * cap, d)
        h1 = jnp.einsum("erd,edf->erf", xe, w1, preferred_element_type=jnp.float32)
        h3 = jnp.einsum("erd,edf->erf", xe, w3, preferred_element_type=jnp.float32)
        h = (jax.nn.silu(h1) * h3).astype(jnp.bfloat16)
        yp = jnp.einsum("erf,efd->erd", h, w2, preferred_element_type=jnp.float32).astype(jnp.bfloat16)
        yp = yp.reshape(el, tp, ep, cap, d).transpose(1, 2, 0, 3, 4)
        parts = lax.all_to_all(yp, "tp", 0, 0, tiled=True)
        y = jnp.sum(parts.astype(jnp.float32), axis=0).astype(jnp.bfloat16)
        back = lax.all_to_all(y, "ep", 0, 0, tiled=True).reshape(n_exp * cap, d)
        ysel = back[jnp.minimum(dest, n_exp * cap - 1)].astype(jnp.float32).reshape(t_loc, top, d)
        wgt = jnp.where(keep, g.reshape(-1), 0.0).reshape(t_loc, top, 1)
        return jnp.sum(ysel * wgt, axis=1).astype(jnp.bfloat16)

    return jax.shard_map(local, mesh=mesh,
                         in_specs=(rows, rows, rows, P("ep", None, "tp"), P("ep", None, "tp"), P("ep", "tp", None)),
                         out_specs=rows, check_vma=False)
```

profile of v0, /device:TPU:0, one launch (start us, length us, event | category | flops | bytes accessed | tf_op | source)
XLA Modules:
  0.0 312.3 jit_solution(2567336580109640597)
XLA Ops:
  6.5 0.0 copy-start
  6.5 0.0 all-gather.3.cloned.1.call-start
  6.5 0.8 copy.23
  7.3 0.1 eq.29
  7.4 0.1 eq.25
  7.5 0.7 broadcast_multiply_fusion
  8.2 0.6 reduce-window.6
  8.8 0.2 slice_reduce_fusion
  9.1 0.1 copy.26
  9.1 0.1 mul.37
  9.2 0.1 fusion.6
  9.4 0.0 copy-done
  9.4 2.8 scatter_custom_fusion
  12.2 30.2 %all_to_all.15 = bf16[2,32,8,2048]{3,2,1,0:T(8,128)(2,1)} all-to-all(bf16[2,32,8,2048]{3,2,1,0:T(8,128)(2,1)S(1)} %bitcast.46), channel_id=1, replica_groups=mesh['dp'=1,'ep'=2,'tp'=4] {'ep'}, dimensions={0} | all-to-all | bytes 4194304 | tf_op jit(solution)/shard_map/all_to_all | solution.py:30
  42.4 0.0 all-gather.3.cloned.1.call-update
  42.4 56.0 %all-gather.3.cloned.1.call-done = bf16[8,32,8,2048]{3,2,1,0:T(8,128)(2,1)} async-done(((bf16[2,32,8,2048]{3,2,1,0:T(8,128)(2,1)}), bf16[8,32,8,2048]{3,2,1,0:T(8,128)(2,1)}) %all-gather.3.cloned.1.call-update) | async-done | bytes 8388624 | tf_op jit(solution)/shard_map/all_gather | solution.py:31
  98.5 8.3 %copy.27 = bf16[4,2,32,8,2048]{4,3,1,0,2:T(8,128)(2,1)} copy(bf16[4,2,32,8,2048]{4,3,2,1,0:T(8,128)(2,1)} %bitcast.45) | data formatting | bytes 16777216 | tf_op jit(solution)/shard_map/all_gather | solution.py:31
  106.7 18.3 %fusion.8 = f32[32,64,256]{2,1,0:T(8,128)S(1)} fusion(bf16[32,64,2048]{2,1,0:T(8,128)(2,1)} %bitcast.40, bf16[32,2048,256]{2,1,0:T(8,128)(2,1)} %param.9), kind=kOutput, calls=%fused_computation.26 | convolution fusion | flops 2147483648 | bytes 44040192 | tf_op jit(solution)/shard_map/erd,edf->erf/dot_general | solution.py:33
  125.1 16.4 %multiply_convert_fusion = bf16[32,64,256]{2,1,0:T(8,128)(2,1)S(1)} fusion(f32[32,64,256]{2,1,0:T(8,128)S(1)} %fusion.8, bf16[32,64,2048]{2,1,0:T(8,128)(2,1)} %bitcast.41, bf16[32,2048,256]{2,1,0:T(8,128)(2,1)} %param.10), kind=kOutput, calls=%fused_computation.6 | convolution fusion | flops 2150629376 | bytes 45088768 | tf_op jit(solution)/shard_map/erd,edf->erf/dot_general | solution.py:34
  141.4 17.1 %convolution_convert_fusion = bf16[32,64,2048]{2,1,0:T(8,128)(2,1)} fusion(bf16[32,64,256]{2,1,0:T(8,128)(2,1)S(1)} %multiply_convert_fusion, bf16[32,256,2048]{2,1,0:T(8,128)(2,1)} %param.11), kind=kOutput, calls=%fused_computation.3 | convolution fusion | flops 2151677952 | bytes 42991616 | tf_op jit(solution)/shard_map/erf,efd->erd/dot_general | solution.py:36
  158.5 8.3 %copy.36 = bf16[32,4,2,8,2048]{4,3,2,0,1:T(8,128)(2,1)} copy(bf16[32,4,2,8,2048]{4,3,2,1,0:T(8,128)(2,1)} %bitcast.44) | data formatting | bytes 16777216 | tf_op jit(solution)/shard_map/reshape | solution.py:37
  166.7 100.3 %all_to_all.16 = bf16[4,2,32,8,2048]{4,3,1,2,0:T(8,128)(2,1)} all-to-all(bf16[4,2,32,8,2048]{4,3,1,2,0:T(8,128)(2,1)} %bitcast.43), channel_id=1, replica_groups=mesh['dp'=1,'ep'=2,'tp'=4] {'tp'}, dimensions={0} | all-to-all | bytes 16777216 | tf_op jit(solution)/shard_map/all_to_all | solution.py:38
  267.0 5.6 %reduce_sum.34 = bf16[2,32,8,2048]{3,2,0,1:T(8,128)(2,1)S(1)} reduce(bf16[4,2,32,8,2048]{4,3,1,2,0:T(8,128)(2,1)} %all_to_all.16, bf16[]{:T(256)} %constant.8.clone.1), dimensions={0}, to_apply=%region_4.5 | reduce | flops 3145728 | bytes 10485762 | tf_op jit(solution)/shard_map/reduce_sum | solution.py:39
  272.6 0.0 copy-start.1
  272.7 1.5 copy.30
  274.1 3.8 %all-to-all-start.2 = ((bf16[2,32,8,2048]{3,2,1,0:T(8,128)(2,1)}), bf16[2,32,8,2048]{3,2,1,0:T(8,128)(2,1)S(1)}, u32[]{:S(2)}, u32[]{:S(2)}) async-start(bf16[2,32,8,2048]{3,2,1,0:T(8,128)(2,1)} %copy.30), calls=%async_computation.2 | async-start | bytes 4194304 | tf_op jit(solution)/shard_map/all_to_all | solution.py:40
  277.9 0.1 lt.45
  278.0 0.0 copy-done.2
  278.0 0.1 copy.31
  278.1 24.3 %all-to-all-done.2 = bf16[2,32,8,2048]{3,2,1,0:T(8,128)(2,1)S(1)} async-done(((bf16[2,32,8,2048]{3,2,1,0:T(8,128)(2,1)}), bf16[2,32,8,2048]{3,2,1,0:T(8,128)(2,1)S(1)}, u32[]{:S(2)}, u32[]{:S(2)}) %all-to-all-start.2) | async-done | bytes 2097184 | tf_op jit(solution)/shard_map/all_to_all | solution.py:40
  302.4 1.4 gather_fusion
  303.8 1.6 fusion
  (10 shorter events, 0.1 us)
Async XLA Ops:
  6.5 2.8 copy-start
  6.5 91.9 %all-gather.3.cloned.1.call-start = ((), (), s32[]{:S(2)}) async-start(), calls=%async_computation.3 | async-start | bytes 10485760 | tf_op jit(solution)/shard_map/all_gather | solution.py:31
  267.0 11.0 %copy-start.2 = (f32[32,8]{0,1:T(8,128)S(1)}, f32[32,8]{0,1:T(8,128)}, u32[]{:S(2)}) copy-start(f32[32,8]{0,1:T(8,128)} %param.8) | copy-start | bytes 3076
  272.6 32.8 %copy-start.1 = (bf16[32,2048]{1,0:T(8,128)(2,1)S(1)}, bf16[32,2048]{1,0:T(8,128)(2,1)}, u32[]{:S(2)}) copy-start(bf16[32,2048]{1,0:T(8,128)(2,1)} %param.6) | copy-start | bytes 393220
  274.1 28.3 %all-to-all-start.2 = ((bf16[2,32,8,2048]{3,2,1,0:T(8,128)(2,1)}), bf16[2,32,8,2048]{3,2,1,0:T(8,128)(2,1)S(1)}, u32[]{:S(2)}, u32[]{:S(2)}) async-start(bf16[2,32,8,2048]{3,2,1,0:T(8,128)(2,1)} %copy.30), calls=%async_computation.2 | async-start | bytes 4194304 | tf_op jit(solution)/shard_map/all_to_all | solution.py:40
Sparse Core Ops, SparseCore 0:
  42.6 55.8 all-gather.2
where the time goes:
time: 313 us; the launch traced here: 312 us
  blocking collectives  131 us (42%)
  waiting for transfers between devices  80.4 us (26%)
  matrix products  51.7 us (17%)
  local copies, waits for them, and re-layouts  23.7 us (8%)
  between operations  13.5 us (4%)
  other arithmetic  8.7 us (3%)
  starting transfers between devices  3.76 us (1%)
    all_to_all x1, blocking collectives, local(): parts = lax.all_to_all(yp, 'tp', 0, 0, tiled=True)  100 us
    all_gather x1, waiting for transfers between devices, local(): allr = lax.all_gather(recv, 'tp', axis=0)  56 us
    all_to_all x1, blocking collectives, local(): recv = lax.all_to_all(buf, 'ep', 0, 0, tiled=True)  30.2 us
    all_to_all x1, waiting for transfers between devices, local(): back = lax.all_to_all(y, 'ep', 0, 0, tiled=True).reshape(n_exp * cap, d)  24.3 us
    dot_general x1, matrix products, local(): h1 = jnp.einsum('erd,edf->erf', xe, w1, preferred_element_type=jnp.float32)  18.3 us
    dot_general x1, matrix products, local(): jnp.einsum('erf,efd->erd', h, w2, preferred_element_type=jnp.float32)  17.1 us
    dot_general x1, matrix products, local(): h3 = jnp.einsum('erd,edf->erf', xe, w3, preferred_element_type=jnp.float32)  16.4 us
    reshape x1, local copies, waits for them, and re-layouts, local(): yp = yp.reshape(el, tp, ep, cap, d).transpose(1, 2, 0, 3, 4)  8.26 us
  transfers between devices with their start and end apart: 2, of which 2 were waited for; matrix products, arithmetic and copies ran while one was open for 0% of the time, Pallas kernels for 0%

commit v1 on v0

v1 whole, which is shorter than its diff:
```python
import functools

import jax
import jax.numpy as jnp
from jax import lax
from jax.experimental import pallas as pl
from jax.experimental.pallas import tpu as pltpu
from jax.sharding import PartitionSpec as P

CF = 2
NS = 20
CW = 512
GE = 8
F32, BF16 = jnp.float32, jnp.bfloat16


def _dot(a, b):
    return jnp.dot(a, b, preferred_element_type=F32)


def _kernel(n_el, cap, x_ref, idx_ref, g_ref, w1_ref, w3_ref, w2_ref, o_ref,
            xall, idxv, gv, gall, xg, ring, hbuf, gt, pt, ybuf, yacc, yrecv, ssum, rfin,
            in_sem, wsem, xs_sem, xr_sem, xf_sem, xp_sem, gs_sem, gr_sem, gf_sem, gp_sem,
            ys_sem, yr_sem, zs_sem, zr_sem):
    ep, tp = lax.axis_index("ep"), lax.axis_index("tp")
    dp = lax.axis_index("dp")
    core = lax.rem(tp, 2)
    chip = ep * 2 + tp // 2
    t_loc, d = x_ref.shape
    top = idx_ref.shape[1]
    n_exp = 2 * n_el
    n_chunk = d // CW
    n_grp = n_el // GE
    n_item = n_el + n_chunk * n_grp
    kt, kd = w1_ref.shape[1], w1_ref.shape[2]
    fl = w1_ref.shape[3]

    def dev(r, flip):
        e2 = 1 - ep if r & 2 else ep
        x2 = 1 - tp // 2 if r & 1 else tp // 2
        c2 = 1 - core if flip else core
        return (dp, e2, x2 * 2 + c2)

    def chip_of(r):
        e2 = 1 - ep if r & 2 else ep
        x2 = 1 - tp // 2 if r & 1 else tp // 2
        return e2 * 2 + x2

    def remote(src, dst, ss, rs, to):
        return pltpu.make_async_remote_copy(src_ref=src, dst_ref=dst, send_sem=ss, recv_sem=rs, device_id=to,
                                            device_id_type=pl.DeviceIdType.MESH)

    def w13_copies(e, slot):
        return (pltpu.make_async_copy(w1_ref.at[e], ring.at[slot, :, :, pl.ds(0, fl)], wsem.at[slot, 0]),
                pltpu.make_async_copy(w3_ref.at[e], ring.at[slot, :, :, pl.ds(fl, fl)], wsem.at[slot, 1]))

    def w2_copies(b, slot):
        c, q = b // n_grp, b % n_grp
        half = GE // 2
        col = pl.multiple_of(c * CW, CW)
        return tuple(
            pltpu.make_async_copy(w2_ref.at[pl.ds(q * GE + s * half, half), :, pl.ds(col, CW)],
                                  ring.at[slot, pl.ds(s * half, half)], wsem.at[slot, s])
            for s in range(2))

    def start_item(i):
        slot = lax.rem(i, NS)

        @pl.when(i < n_el)
        def _():
            for c in w13_copies(i, slot):
                c.start()

        @pl.when(jnp.logical_and(i >= n_el, i < n_item))
        def _():
            for c in w2_copies(i - n_el, slot):
                c.start()

    mine = xall.at[chip, pl.ds(core * t_loc, t_loc)]
    x_in = pltpu.make_async_copy(x_ref, mine, in_sem.at[0])
    i_in = pltpu.make_async_copy(idx_ref, idxv, in_sem.at[1])
    g_in = pltpu.make_async_copy(g_ref, gv, in_sem.at[2])
    x_in.start()
    i_in.start()
    g_in.start()
    barrier = pltpu.get_barrier_semaphore()
    peers = [(1, False), (2, False), (3, False), (0, True)]
    for r, flip in peers:
        pl.semaphore_signal(barrier, inc=1, device_id=dev(r, flip), device_id_type=pl.DeviceIdType.MESH)

    def prime(i, _):
        start_item(i)
        return 0

    lax.fori_loop(0, NS, prime, 0)
    x_in.wait()
    i_in.wait()
    g_in.wait()
    pl.semaphore_wait(barrier, len(peers))

    def x_copy(r, flip):
        return remote(mine, mine, xs_sem.at[r], xp_sem.at[0] if flip else xr_sem.at[r], dev(r, flip))

    for r in (3, 1, 2):
        x_copy(r, False).start()
    x_copy(0, True).start()

    ids, gates = idxv[...], gv[...]
    lane = lax.broadcasted_iota(jnp.int32, (t_loc, 2 * n_exp), 1)
    e_of = lax.rem(lane, n_exp)
    gd = jnp.zeros((t_loc, 2 * n_exp), F32)
    hit = jnp.zeros((t_loc, 2 * n_exp), F32)
    for j in range(top):
        eq = ids[:, j:j + 1] == e_of
        gd = jnp.where(eq, gates[:, j:j + 1], gd)
        hit = jnp.where(eq, 1.0, hit)
    before = (lax.broadcasted_iota(jnp.int32, (t_loc, t_loc), 1)
              < lax.broadcasted_iota(jnp.int32, (t_loc, t_loc), 0)).astype(BF16)
    slot = _dot(before, hit.astype(BF16))
    keep = jnp.logical_and(hit > 0.5, slot < cap - 0.5)
    gall[chip, pl.ds(core * t_loc, t_loc)] = jnp.where(keep, jnp.where(lane < n_exp, gd, slot),
                                                       jnp.where(lane < n_exp, 0.0, -1.0))
    gmine = gall.at[chip, pl.ds(core * t_loc, t_loc)]

    def g_copy(r, flip):
        return remote(gmine, gmine, gs_sem.at[r], gp_sem.at[0] if flip else gr_sem.at[r], dev(r, flip))

    for r in (3, 1, 2):
        g_copy(r, False).start()
    g_copy(0, True).start()

    def fwd(buf, ss, ps, r):
        ref = buf.at[chip_of(r), pl.ds(core * t_loc, t_loc)]
        return remote(ref, ref, ss.at[r], ps.at[r], dev(0, True))

    def arrived(buf, ps, r):
        ref = buf.at[chip_of(r), pl.ds((1 - core) * t_loc, t_loc)]
        return remote(ref, ref, xs_sem.at[0], ps.at[r], dev(0, True))

    def landed(buf, rs, r):
        ref = buf.at[chip_of(r), pl.ds(core * t_loc, t_loc)]
        return remote(ref, ref, xs_sem.at[0], rs.at[r], dev(r, False))

    pair = 2 * t_loc
    nk = n_el * 2 * cap
    el = lax.broadcasted_iota(jnp.int32, (2 * n_exp, nk), 1) // (2 * cap) + ep * n_el
    row = lax.broadcasted_iota(jnp.int32, (2 * n_exp, nk), 0)
    ex_g = (row == el).astype(BF16)
    ex_s = (row == el + n_exp).astype(BF16)
    kl = lax.broadcasted_iota(jnp.int32, (pair, nk), 1)
    tr = lax.broadcasted_iota(jnp.int32, (pair, nk), 0)
    same_core = lax.rem(kl // cap, 2) == tr // t_loc
    s_of = lax.rem(kl, cap).astype(F32)

    def dispatch(r):
        q = chip_of(r)
        gs = gall[q]
        hi = gs.astype(BF16)
        r1 = gs - hi.astype(F32)
        mid = r1.astype(BF16)
        lo = (r1 - mid.astype(F32)).astype(BF16)
        here = jnp.logical_and(_dot(hi, ex_s) == s_of, same_core)
        for k, part in enumerate((hi, mid, lo)):
            gt[q, pl.ds(k * pair, pair)] = jnp.where(here, _dot(part, ex_g), 0.0).astype(BF16)
        pt[...] = jnp.where(here, 1.0, 0.0).T.astype(BF16)
        for c in range(d // CW):
            rows = _dot(pt[...], xall[q, :, c * CW:(c + 1) * CW])
            xg[:, q, :, c * CW:(c + 1) * CW] = rows.astype(BF16).reshape(n_el, 2 * cap, CW)

    for r in (0, 1, 2, 3):
        if r:
            landed(xall, xr_sem, r).wait_recv()
            fwd(xall, xf_sem, xp_sem, r).start()
            landed(gall, gr_sem, r).wait_recv()
            fwd(gall, gf_sem, gp_sem, r).start()
    for r in (0, 1, 2, 3):
        arrived(xall, xp_sem, r).wait_recv()
        arrived(gall, gp_sem, r).wait_recv()
        dispatch(r)

    m = 8 * cap

    def wait13(e):
        for c in w13_copies(e, lax.rem(e, NS)):
            c.wait()

    def up(k, _):
        e0 = 2 * k
        wait13(e0)
        wait13(e0 + 1)
        acc = []
        for j in range(2):
            w = ring[lax.rem(e0 + j, NS)].reshape(kt * kd, 2 * fl)
            acc.append(_dot(xg[e0 + j].reshape(m, d), w))
        for j in range(2):
            a, b = acc[j][:, :fl], acc[j][:, fl:]
            hbuf[e0 + j] = (a * jax.nn.sigmoid(a) * b).astype(BF16)
        start_item(e0 + NS)
        start_item(e0 + 1 + NS)
        return 0

    lax.fori_loop(0, n_el // 2, up, 0)

    def y_copy(c):
        return remote(yacc.at[c, 1 - core], yrecv.at[c], ys_sem.at[c], yr_sem.at[c], dev(0, True))

    def z_copy(c, r):
        return remote(ssum.at[c, chip_of(r)], rfin.at[c, chip], zs_sem.at[c, r], zr_sem.at[c, r], dev(r, False))

    def z_landed(c, r):
        return remote(ssum.at[c, chip_of(r)], rfin.at[c, chip_of(r)], zs_sem.at[c, r], zr_sem.at[c, r], dev(r, False))

    def second(c):
        y_copy(c).wait_recv()
        ssum[c] = yacc[c, core] + yrecv[c]
        for r in (3, 1, 2):
            z_copy(c, r).start()

    def down(b, _):
        c, q = b // n_grp, b % n_grp
        slot = lax.rem(b + n_el, NS)
        for cp in w2_copies(b, slot):
            cp.wait()
        for j in range(GE):
            y = _dot(hbuf[q * GE + j], ring[slot, j])
            ybuf[q * GE + j] = y.astype(BF16).reshape(4, 2 * cap, CW)
        start_item(b + n_el + NS)

        @pl.when(jnp.logical_and(q == 1, c > 0))
        def _():
            second(c - 1)

        @pl.when(q == n_grp - 1)
        def _():
            for p in range(4):
                z = _dot(gt[p], ybuf[:, p].reshape(nk, CW))
                z = z[:pair] + z[pair:2 * pair] + z[2 * pair:]
                for k in range(2):
                    yacc[c, k, p] = z[k * t_loc:(k + 1) * t_loc]
            y_copy(c).start()

        return 0

    lax.fori_loop(0, n_chunk * n_grp, down, 0)
    second(n_chunk - 1)
    for c in range(n_chunk):
        tot = ssum[c, chip]
        for r in (1, 2, 3):
            z_landed(c, r).wait_recv()
            tot = tot + rfin[c, chip_of(r)]
        o_ref[:, c * CW:(c + 1) * CW] = tot

    for r in (3, 1, 2):
        x_copy(r, False).wait_send()
        g_copy(r, False).wait_send()
        fwd(xall, xf_sem, xp_sem, r).wait_send()
        fwd(gall, gf_sem, gp_sem, r).wait_send()
    x_copy(0, True).wait_send()
    g_copy(0, True).wait_send()
    for c in range(n_chunk):
        y_copy(c).wait_send()
        for r in (1, 2, 3):
            z_copy(c, r).wait_send()


def solution(mesh):
    rows = P(("dp", "ep", "tp"), None)

    def local(x, idx, g, w1, w3, w2):
        t_loc, d = x.shape
        top = idx.shape[1]
        el, _, fl = w1.shape
        n_exp = 2 * el
        cap = CF * top * t_loc // n_exp
        nc = d // CW
        nk = el * 2 * cap
        dma, vm = pltpu.SemaphoreType.DMA, pltpu.VMEM
        any_ = pl.BlockSpec(memory_space=pl.ANY)
        y = pl.pallas_call(
            functools.partial(_kernel, el, cap),
            out_shape=jax.ShapeDtypeStruct((t_loc, d), F32),
            in_specs=[any_] * 6,
            out_specs=pl.BlockSpec(memory_space=pltpu.VMEM),
            scratch_shapes=[
                vm((4, 2 * t_loc, d), BF16),
                vm((t_loc, top), jnp.int32),
                vm((t_loc, top), F32),
                vm((4, 2 * t_loc, 2 * n_exp), F32),
                vm((el, 4, 2 * cap, d), BF16),
                vm((NS, d // fl, fl, 2 * fl), BF16),
                vm((el, 8 * cap, fl), BF16),
                vm((4, 6 * t_loc, nk), BF16),
                vm((nk, 2 * t_loc), BF16),
                vm((el, 4, 2 * cap, CW), BF16),
                vm((nc, 2, 4, t_loc, CW), F32),
                vm((nc, 4, t_loc, CW), F32),
                vm((nc, 4, t_loc, CW), F32),
                vm((nc, 4, t_loc, CW), F32),
                dma((3,)), dma((NS, 2)),
                dma((4,)), dma((4,)), dma((4,)), dma((4,)),
                dma((4,)), dma((4,)), dma((4,)), dma((4,)),
                dma((nc,)), dma((nc,)), dma((nc, 4)), dma((nc, 4)),
            ],
            compiler_params=pltpu.CompilerParams(collective_id=0, has_side_effects=True,
                                                 vmem_limit_bytes=67043328),
            name="moe",
        )(x, idx, g, w1.reshape(el, d // fl, fl, fl), w3.reshape(el, d // fl, fl, fl), w2)
        return y.astype(BF16)

    return jax.shard_map(local, mesh=mesh,
                         in_specs=(rows, rows, rows, P("ep", None, "tp"), P("ep", None, "tp"), P("ep", "tp", None)),
                         out_specs=rows, check_vma=False)
```

time: 313 us -> 53.4 us (0.17)
  blocking collectives: 131 us -> 0 us
  waiting for transfers between devices: 80.4 us -> 0 us
  matrix products: 51.7 us -> 0 us
  Pallas kernels: 0 us -> 48.8 us
  local copies, waits for them, and re-layouts: 23.7 us -> 2.72 us
  between operations: 13.5 us -> 0.01 us
  other arithmetic: 8.7 us -> 1.62 us
  starting transfers between devices: 3.76 us -> 0 us
    all_to_all x2 -> x0, blocking collectives: 131 us -> none  [the longest x1 100 us: local(): parts = lax.all_to_all(yp, 'tp', 0, 0, tiled=True)]
    all_gather x1 -> x0, waiting for transfers between devices: 56 us -> none  [local(): allr = lax.all_gather(recv, 'tp', axis=0)]
    dot_general x3 -> x0, matrix products: 51.7 us -> none  [the longest x1 18.3 us: local(): h1 = jnp.einsum('erd,edf->erf', xe, w1, preferred_element_type=jnp.float32)]
    pallas_call x0 -> x1, Pallas kernels: none -> 48.8 us  [local(): pl.pallas_call(functools.partial(_kernel, el, cap), out_shape=jax.ShapeDt...]
    all_to_all x1 -> x0, waiting for transfers between devices: 24.3 us -> none  [local(): back = lax.all_to_all(y, 'ep', 0, 0, tiled=True).reshape(n_exp * cap, d)]
    reshape x1 -> x0, local copies, waits for them, and re-layouts: 8.26 us -> none  [local(): yp = yp.reshape(el, tp, ep, cap, d).transpose(1, 2, 0, 3, 4)]
    all_gather x1 -> x0, local copies, waits for them, and re-layouts: 8.25 us -> none  [local(): allr = lax.all_gather(recv, 'tp', axis=0)]
    reduce_sum x3 -> x0, other arithmetic: 7.32 us -> none  [the longest x1 5.59 us: local(): y = jnp.sum(parts.astype(jnp.float32), axis=0).astype(jnp.bfloat16)]
  transfers between devices with their start and end apart: 2 -> 0, of which waited for: 2 -> 0; matrix products, arithmetic and copies ran while one was open for 0% -> 0% of each run, Pallas kernels for 0% -> 0%
where the time goes in v1:
time: 53.4 us; the launch traced here: 53.2 us
  Pallas kernels  48.8 us (91%)
  local copies, waits for them, and re-layouts  2.72 us (5%)
  other arithmetic  1.62 us (3%)
    pallas_call x1, Pallas kernels, local(): pl.pallas_call(functools.partial(_kernel, el, cap), out_shape=jax.ShapeDt...  48.8 us
    unnamed x2, local copies, waits for them, and re-layouts  2.72 us
    convert_element_type x1, other arithmetic, local(): return y.astype(BF16)  1.62 us

profile of v1, /device:TPU:0, one launch (start us, length us, event | category | flops | bytes accessed | tf_op | source)
XLA Modules:
  0.0 53.2 jit_solution(6474907785943089852)
XLA Ops:
  0.0 1.4 %copy.7.idx_ref = s32[32,8]{1,0:T(8,128)} copy(s32[32,8]{0,1:T(8,128)} %param.7) | data formatting | bytes 2048 | tf_op args[1]
  1.4 1.4 %copy.8.g_ref = f32[32,8]{1,0:T(8,128)} copy(f32[32,8]{0,1:T(8,128)} %param.8) | data formatting | bytes 2048 | tf_op args[2]
  2.7 48.8 %moe.1 = f32[32,2048]{1,0:T(8,128)} custom-call(bf16[32,2048]{1,0:T(8,128)(2,1)} %x_ref.1, s32[32,8]{1,0:T(8,128)} %copy.7.idx_ref, f32[32,8]{1,0:T(8,128)} %copy.8.g_ref, bf16[32,8,256,256]{3,2,1,0:T(8,128)(2,1)} %bitcast.2, bf16[32,8,256,256]{3,2,1,0:T(8,128)(2,1)} %bitcast.3, bf16[32,256,2048]{2,1,0:T(8,128)(2,1)} %w2_ref.1), custom_call_target="tpu_custom_call" | custom-call | tf_op jit(solution)/shard_map/moe/pallas_call | solution.py:279
  51.6 1.6 %convert_element_type.3 = bf16[32,2048]{1,0:T(8,128)(2,1)} convert(f32[32,2048]{1,0:T(8,128)} %moe.1) | non-fusion elementwise | flops 65536 | bytes 393216 | tf_op jit(solution)/shard_map/convert_element_type | solution.py:308

commit v2 on v1

--- a/solution.py
+++ b/solution.py
@@ -9,6 +9,7 @@
 
 CF = 2
 NS = 20
+PRIME = (4, 12, 16, 18, NS)
 CW = 512
 GE = 8
 F32, BF16 = jnp.float32, jnp.bfloat16
@@ -27,7 +28,7 @@
     core = lax.rem(tp, 2)
     chip = ep * 2 + tp // 2
     t_loc, d = x_ref.shape
-    top = idx_ref.shape[1]
+    top = idx_ref.shape[0]
     n_exp = 2 * n_el
     n_chunk = d // CW
     n_grp = n_el // GE
@@ -92,7 +93,7 @@
         start_item(i)
         return 0
 
-    lax.fori_loop(0, NS, prime, 0)
+    lax.fori_loop(0, PRIME[0], prime, 0)
     x_in.wait()
     i_in.wait()
     g_in.wait()
@@ -106,20 +107,21 @@
     x_copy(0, True).start()
 
     ids, gates = idxv[...], gv[...]
-    lane = lax.broadcasted_iota(jnp.int32, (t_loc, 2 * n_exp), 1)
-    e_of = lax.rem(lane, n_exp)
-    gd = jnp.zeros((t_loc, 2 * n_exp), F32)
-    hit = jnp.zeros((t_loc, 2 * n_exp), F32)
+    line = lax.broadcasted_iota(jnp.int32, (2 * n_exp, t_loc), 0)
+    e_of = lax.rem(line, n_exp)
+    gd = jnp.zeros((2 * n_exp, t_loc), F32)
+    hit = jnp.zeros((2 * n_exp, t_loc), F32)
     for j in range(top):
-        eq = ids[:, j:j + 1] == e_of
-        gd = jnp.where(eq, gates[:, j:j + 1], gd)
+        eq = ids[j:j + 1] == e_of
+        gd = jnp.where(eq, gates[j:j + 1], gd)
         hit = jnp.where(eq, 1.0, hit)
-    before = (lax.broadcasted_iota(jnp.int32, (t_loc, t_loc), 1)
-              < lax.broadcasted_iota(jnp.int32, (t_loc, t_loc), 0)).astype(BF16)
-    slot = _dot(before, hit.astype(BF16))
+    before = (lax.broadcasted_iota(jnp.int32, (t_loc, t_loc), 0)
+              < lax.broadcasted_iota(jnp.int32, (t_loc, t_loc), 1)).astype(BF16)
+    slot = _dot(hit.astype(BF16), before)
     keep = jnp.logical_and(hit > 0.5, slot < cap - 0.5)
-    gall[chip, pl.ds(core * t_loc, t_loc)] = jnp.where(keep, jnp.where(lane < n_exp, gd, slot),
-                                                       jnp.where(lane < n_exp, 0.0, -1.0))
+    table = jnp.where(keep, jnp.where(line < n_exp, gd, slot), jnp.where(line < n_exp, 0.0, -1.0))
+    gall[chip, pl.ds(core * t_loc, t_loc)] = table.T
+    lax.fori_loop(PRIME[0], PRIME[1], prime, 0)
     gmine = gall.at[chip, pl.ds(core * t_loc, t_loc)]
 
     def g_copy(r, flip):
@@ -167,16 +169,20 @@
             rows = _dot(pt[...], xall[q, :, c * CW:(c + 1) * CW])
             xg[:, q, :, c * CW:(c + 1) * CW] = rows.astype(BF16).reshape(n_el, 2 * cap, CW)
 
-    for r in (0, 1, 2, 3):
-        if r:
-            landed(xall, xr_sem, r).wait_recv()
-            fwd(xall, xf_sem, xp_sem, r).start()
-            landed(gall, gr_sem, r).wait_recv()
-            fwd(gall, gf_sem, gp_sem, r).start()
-    for r in (0, 1, 2, 3):
+    def settle(r):
         arrived(xall, xp_sem, r).wait_recv()
         arrived(gall, gp_sem, r).wait_recv()
         dispatch(r)
+
+    settle(0)
+    for k, r in enumerate((2, 3, 1)):
+        landed(xall, xr_sem, r).wait_recv()
+        fwd(xall, xf_sem, xp_sem, r).start()
+        landed(gall, gr_sem, r).wait_recv()
+        fwd(gall, gf_sem, gp_sem, r).start()
+        lax.fori_loop(PRIME[k + 1], PRIME[k + 2], prime, 0)
+    for r in (2, 3, 1):
+        settle(r)
 
     m = 8 * cap
 
@@ -283,8 +289,8 @@
             out_specs=pl.BlockSpec(memory_space=pltpu.VMEM),
             scratch_shapes=[
                 vm((4, 2 * t_loc, d), BF16),
-                vm((t_loc, top), jnp.int32),
-                vm((t_loc, top), F32),
+                vm((top, t_loc), jnp.int32),
+                vm((top, t_loc), F32),
                 vm((4, 2 * t_loc, 2 * n_exp), F32),
                 vm((el, 4, 2 * cap, d), BF16),
                 vm((NS, d // fl, fl, 2 * fl), BF16),
@@ -304,7 +310,7 @@
             compiler_params=pltpu.CompilerParams(collective_id=0, has_side_effects=True,
                                                  vmem_limit_bytes=67043328),
             name="moe",
-        )(x, idx, g, w1.reshape(el, d // fl, fl, fl), w3.reshape(el, d // fl, fl, fl), w2)
+        )(x, idx.T, g.T, w1.reshape(el, d // fl, fl, fl), w3.reshape(el, d // fl, fl, fl), w2)
         return y.astype(BF16)
 
     return jax.shard_map(local, mesh=mesh,

time: 53.4 us -> 50.3 us (0.942)
  local copies, waits for them, and re-layouts: 2.72 us -> 0 us
    unnamed x2 -> x0, local copies, waits for them, and re-layouts: 2.72 us -> none
where the time goes in v2:
time: 50.3 us; the launch traced here: 50.2 us
  Pallas kernels  48.5 us (96%)
  other arithmetic  1.62 us (3%)
    pallas_call x1, Pallas kernels, local(): pl.pallas_call(functools.partial(_kernel, el, cap), out_shape=jax.ShapeDt...  48.5 us
    convert_element_type x1, other arithmetic, local(): return y.astype(BF16)  1.62 us

profile of v2, /device:TPU:0, one launch (start us, length us, event | category | flops | bytes accessed | tf_op | source)
XLA Modules:
  0.0 50.2 jit_solution(17338729760982873186)
XLA Ops:
  0.0 48.5 %moe.1 = f32[32,2048]{1,0:T(8,128)} custom-call(bf16[32,2048]{1,0:T(8,128)(2,1)} %x_ref.1, s32[8,32]{1,0:T(8,128)} %bitcast.6, f32[8,32]{1,0:T(8,128)} %bitcast.7, bf16[32,8,256,256]{3,2,1,0:T(8,128)(2,1)} %bitcast.4, bf16[32,8,256,256]{3,2,1,0:T(8,128)(2,1)} %bitcast.5, bf16[32,256,2048]{2,1,0:T(8,128)(2,1)} %w2_ref.1), custom_call_target="tpu_custom_call" | custom-call | tf_op jit(solution)/shard_map/moe/pallas_call | solution.py:285
  48.6 1.6 %convert_element_type.3 = bf16[32,2048]{1,0:T(8,128)(2,1)} convert(f32[32,2048]{1,0:T(8,128)} %moe.1) | non-fusion elementwise | flops 65536 | bytes 393216 | tf_op jit(solution)/shard_map/convert_element_type | solution.py:314

commit v3 on v2

v3 whole, which is shorter than its diff:
```python
import functools

import jax
import jax.numpy as jnp
from jax import lax
from jax.experimental import pallas as pl
from jax.experimental.pallas import tpu as pltpu
from jax.sharding import PartitionSpec as P

CF = 2
NS = 20
PRIME = (4, 12, NS)
KW = 512
NW = 8
UP = 4
CW = 256
GE = 16
F32, BF16 = jnp.float32, jnp.bfloat16


def _dot(a, b):
    return jnp.dot(a, b, preferred_element_type=F32)


def _kernel(n_el, cap, x_ref, idx_ref, g_ref, w1_ref, w3_ref, w2_ref, o_ref,
            xall, idxv, gv, sall, gall, xg, ring, acc, hbuf, gt, pt, ybuf, yacc, yrecv, ssum, rfin,
            in_sem, wsem, xs_sem, xr_sem, xf_sem, xp_sem, ss_sem, sr_sem, sf_sem, sp_sem, gs_sem, gr_sem, gf_sem, gp_sem,
            ys_sem, yr_sem, zs_sem, zr_sem):
    ep, tp = lax.axis_index("ep"), lax.axis_index("tp")
    dp = lax.axis_index("dp")
    core = lax.rem(tp, 2)
    chip = ep * 2 + tp // 2
    t_loc, d = x_ref.shape
    top = idx_ref.shape[0]
    n_exp = 2 * n_el
    n_chunk = d // CW
    n_grp = n_el // GE
    n_item = n_el + n_chunk * n_grp
    kt, kd = w1_ref.shape[1], w1_ref.shape[2]
    fl = w1_ref.shape[3]
    n_k = d // KW
    rows = pl.ds(core * t_loc, t_loc)
    other = pl.ds((1 - core) * t_loc, t_loc)

    def dev(r, flip):
        e2 = 1 - ep if r & 2 else ep
        x2 = 1 - tp // 2 if r & 1 else tp // 2
        c2 = 1 - core if flip else core
        return (dp, e2, x2 * 2 + c2)

    def chip_of(r):
        e2 = 1 - ep if r & 2 else ep
        x2 = 1 - tp // 2 if r & 1 else tp // 2
        return e2 * 2 + x2

    def remote(src, dst, ss, rs, to):
        return pltpu.make_async_remote_copy(src_ref=src, dst_ref=dst, send_sem=ss, recv_sem=rs, device_id=to,
                                            device_id_type=pl.DeviceIdType.MESH)

    def w13_copies(e, slot):
        return (pltpu.make_async_copy(w1_ref.at[e], ring.at[slot, :, :, pl.ds(0, fl)], wsem.at[slot, 0]),
                pltpu.make_async_copy(w3_ref.at[e], ring.at[slot, :, :, pl.ds(fl, fl)], wsem.at[slot, 1]))

    def w2_copies(b, slot):
        c, q = b // n_grp, b % n_grp
        half = GE // 2
        col = pl.multiple_of(c * CW, CW)
        return tuple(
            pltpu.make_async_copy(w2_ref.at[pl.ds(q * GE + s * half, half), :, pl.ds(col, CW)],
                                  ring.at[slot, :, :, pl.ds(s * CW, CW)], wsem.at[slot, s])
            for s in range(2))

    def start_item(i):
        slot = lax.rem(i, NS)

        @pl.when(i < n_el)
        def _():
            for c in w13_copies(i, slot):
                c.start()

        @pl.when(jnp.logical_and(i >= n_el, i < n_item))
        def _():
            for c in w2_copies(i - n_el, slot):
                c.start()

    def prime(i, _):
        start_item(i)
        return 0

    x_in = [pltpu.make_async_copy(x_ref.at[:, pl.ds(k * KW, KW)], xall.at[k, chip, rows], in_sem.at[2 + k])
            for k in range(n_k)]
    i_in = pltpu.make_async_copy(idx_ref, idxv, in_sem.at[0])
    g_in = pltpu.make_async_copy(g_ref, gv, in_sem.at[1])
    i_in.start()
    g_in.start()
    for c in x_in:
        c.start()
    barrier = pltpu.get_barrier_semaphore()
    peers = [(1, False), (2, False), (3, False), (0, True)]
    for r, flip in peers:
        pl.semaphore_signal(barrier, inc=1, device_id=dev(r, flip), device_id_type=pl.DeviceIdType.MESH)
    lax.fori_loop(0, PRIME[0], prime, 0)
    i_in.wait()
    g_in.wait()

    ids, gates = idxv[...], gv[...]
    line = lax.broadcasted_iota(jnp.int32, (2 * n_exp, t_loc), 0)
    gd = jnp.zeros((2 * n_exp, t_loc), F32)
    hit = jnp.zeros((2 * n_exp, t_loc), F32)
    for j in range(top):
        eq = ids[j:j + 1] == line
        gd = jnp.where(eq, gates[j:j + 1], gd)
        hit = jnp.where(eq, 1.0, hit)
    before = (lax.broadcasted_iota(jnp.int32, (t_loc, t_loc), 0)
              < lax.broadcasted_iota(jnp.int32, (t_loc, t_loc), 1)).astype(BF16)
    slot = _dot(hit.astype(BF16), before)
    keep = jnp.logical_and(hit > 0.5, slot < cap - 0.5)
    sall[chip, rows] = jnp.where(keep, slot, -1.0).T.astype(BF16)
    gall[chip, rows] = jnp.where(keep, gd, 0.0).T

    for c in x_in:
        c.wait()
    pl.semaphore_wait(barrier, len(peers))

    class Gather:
        def __init__(self, buf, ss, rs, fs, ps):
            self.buf, self.ss, self.rs, self.fs, self.ps = buf, ss, rs, fs, ps

        def out(self, r):
            ref = self.buf.at[chip, rows]
            return remote(ref, ref, self.ss.at[r], self.rs.at[r] if r else self.ps.at[0], dev(r, r == 0))

        def landed(self, r):
            ref = self.buf.at[chip_of(r), rows]
            return remote(ref, ref, self.ss.at[r], self.rs.at[r], dev(r, False))

        def fwd(self, r):
            ref = self.buf.at[chip_of(r), rows]
            return remote(ref, ref, self.fs.at[r], self.ps.at[r], dev(0, True))

        def arrived(self, r):
            ref = self.buf.at[chip_of(r), other]
            return remote(ref, ref, self.fs.at[r], self.ps.at[r], dev(0, True))

        def send(self):
            for r in (3, 1, 2, 0):
                self.out(r).start()

        def forward(self):
            for r in (2, 3, 1):
                self.landed(r).wait_recv()
                self.fwd(r).start()

        def settle(self):
            for r in (0, 2, 3, 1):
                self.arrived(r).wait_recv()

        def drain(self):
            for r in (3, 1, 2):
                self.out(r).wait_send()
                self.fwd(r).wait_send()
            self.out(0).wait_send()

    xs = [Gather(xall.at[k], xs_sem.at[k], xr_sem.at[k], xf_sem.at[k], xp_sem.at[k]) for k in range(n_k)]
    sg = Gather(sall, ss_sem, sr_sem, sf_sem, sp_sem)
    gg = Gather(gall, gs_sem, gr_sem, gf_sem, gp_sem)
    sg.send()
    for x in xs:
        x.send()
    gg.send()
    lax.fori_loop(PRIME[0], PRIME[1], prime, 0)

    pair = 2 * t_loc
    nk = n_el * 2 * cap
    m = 8 * cap
    el = lax.broadcasted_iota(jnp.int32, (2 * n_exp, nk), 1) // (2 * cap) + ep * n_el
    expand = (lax.broadcasted_iota(jnp.int32, (2 * n_exp, nk), 0) == el).astype(BF16)
    kl = lax.broadcasted_iota(jnp.int32, (pair, nk), 1)
    tr = lax.broadcasted_iota(jnp.int32, (pair, nk), 0)
    want = jnp.where(lax.rem(kl // cap, 2) == tr // t_loc, lax.rem(kl, cap), -2).astype(F32)

    sg.forward()
    sg.settle()
    for q in range(4):
        pt[q] = jnp.where(_dot(sall[q], expand) == want, 1.0, 0.0).T.astype(BF16)
    lax.fori_loop(PRIME[1], PRIME[2], prime, 0)

    def wait13(e):
        for c in w13_copies(e, lax.rem(e, NS)):
            c.wait()

    def swiglu(v):
        a, b = v[:, :fl], v[:, fl:]
        return (a * jax.nn.sigmoid(a) * b).astype(BF16)

    xs[0].forward()
    for k in range(n_k):
        xs[k].settle()
        for q in range(4):
            got = _dot(pt[q], xall[k, q])
            xg[k, :, q] = got.astype(BF16).reshape(n_el, 2 * cap, KW)
        if k + 1 < n_k:
            xs[k + 1].forward()
        else:
            gg.forward()

        def part(u, _, k=k):
            for j in range(UP):
                e = u * UP + j
                if k == 0:
                    wait13(e)
            vals = []
            for j in range(UP):
                e = u * UP + j
                w = ring[lax.rem(e, NS), k * (KW // kd):(k + 1) * (KW // kd)].reshape(KW, 2 * fl)
                vals.append(_dot(xg[k, e].reshape(m, KW), w))
            for j in range(UP):
                e = u * UP + j
                v = vals[j] if k == 0 else acc[e] + vals[j]
                if k + 1 < n_k:
                    acc[e] = v
                else:
                    hbuf[e] = swiglu(v)
            if k + 1 == n_k:
                for j in range(UP):
                    start_item(u * UP + j + NS)
            return 0

        lax.fori_loop(0, NW // UP, part, 0)

    gg.settle()
    for q in range(4):
        here = _dot(sall[q], expand) == want
        gs = gall[q]
        hi = gs.astype(BF16)
        r1 = gs - hi.astype(F32)
        mid = r1.astype(BF16)
        lo = (r1 - mid.astype(F32)).astype(BF16)
        for k, p in enumerate((hi, mid, lo)):
            gt[q, pl.ds(k * pair, pair)] = jnp.where(here, _dot(p, expand), 0.0).astype(BF16)

    def up(u, _):
        for j in range(UP):
            wait13(u * UP + j)
        vals = []
        for j in range(UP):
            e = u * UP + j
            w = ring[lax.rem(e, NS)].reshape(n_k, KW, 2 * fl)
            v = _dot(xg[0, e].reshape(m, KW), w[0])
            for k in range(1, n_k):
                v = v + _dot(xg[k, e].reshape(m, KW), w[k])
            vals.append(v)
        for j in range(UP):
            hbuf[u * UP + j] = swiglu(vals[j])
        for j in range(UP):
            start_item(u * UP + j + NS)
        return 0

    lax.fori_loop(NW // UP, n_el // UP, up, 0)

    def y_copy(c):
        return remote(yacc.at[c, 1 - core], yrecv.at[c], ys_sem.at[c], yr_sem.at[c], dev(0, True))

    def z_copy(c, r):
        return remote(ssum.at[c, chip_of(r)], rfin.at[c, chip], zs_sem.at[c, r], zr_sem.at[c, r], dev(r, False))

    def z_landed(c, r):
        return remote(ssum.at[c, chip_of(r)], rfin.at[c, chip_of(r)], zs_sem.at[c, r], zr_sem.at[c, r], dev(r, False))

    def second(c):
        y_copy(c).wait_recv()
        ssum[c] = yacc[c, core] + yrecv[c]
        for r in (3, 1, 2):
            z_copy(c, r).start()

    def down(b, _):
        c, q = b // n_grp, b % n_grp
        slot = lax.rem(b + n_el, NS)
        for cp in w2_copies(b, slot):
            cp.wait()
        for j in range(GE):
            half = GE // 2
            w = ring[slot, j % half, :, (j // half) * CW:(j // half + 1) * CW]
            ybuf[q * GE + j] = _dot(hbuf[q * GE + j], w).astype(BF16).reshape(4, 2 * cap, CW)
        start_item(b + n_el + NS)

        @pl.when(jnp.logical_and(q == 0, c > 0))
        def _():
            second(c - 1)

        @pl.when(q == n_grp - 1)
        def _():
            for p in range(4):
                z = _dot(gt[p], ybuf[:, p].reshape(nk, CW))
                z = z[:pair] + z[pair:2 * pair] + z[2 * pair:]
                for k in range(2):
                    yacc[c, k, p] = z[k * t_loc:(k + 1) * t_loc]
            y_copy(c).start()

        return 0

    lax.fori_loop(0, n_chunk * n_grp, down, 0)
    second(n_chunk - 1)
    for c in range(n_chunk):
        tot = ssum[c, chip]
        for r in (1, 2, 3):
            z_landed(c, r).wait_recv()
            tot = tot + rfin[c, chip_of(r)]
        o_ref[:, c * CW:(c + 1) * CW] = tot

    for x in xs + [sg, gg]:
        x.drain()
    for c in range(n_chunk):
        y_copy(c).wait_send()
        for r in (1, 2, 3):
            z_copy(c, r).wait_send()


def solution(mesh):
    rows = P(("dp", "ep", "tp"), None)

    def local(x, idx, g, w1, w3, w2):
        t_loc, d = x.shape
        top = idx.shape[1]
        el, _, fl = w1.shape
        n_exp = 2 * el
        cap = CF * top * t_loc // n_exp
        nc = d // CW
        nk = el * 2 * cap
        dma, vm = pltpu.SemaphoreType.DMA, pltpu.VMEM
        any_ = pl.BlockSpec(memory_space=pl.ANY)
        y = pl.pallas_call(
            functools.partial(_kernel, el, cap),
            out_shape=jax.ShapeDtypeStruct((t_loc, d), F32),
            in_specs=[any_] * 6,
            out_specs=pl.BlockSpec(memory_space=pltpu.VMEM),
            scratch_shapes=[
                vm((d // KW, 4, 2 * t_loc, KW), BF16),
                vm((top, t_loc), jnp.int32),
                vm((top, t_loc), F32),
                vm((4, 2 * t_loc, 2 * n_exp), BF16),
                vm((4, 2 * t_loc, 2 * n_exp), F32),
                vm((d // KW, el, 4, 2 * cap, KW), BF16),
                vm((NS, d // fl, fl, 2 * fl), BF16),
                vm((NW, 8 * cap, 2 * fl), F32),
                vm((el, 8 * cap, fl), BF16),
                vm((4, 6 * t_loc, nk), BF16),
                vm((4, nk, 2 * t_loc), BF16),
                vm((el, 4, 2 * cap, CW), BF16),
                vm((nc, 2, 4, t_loc, CW), F32),
                vm((nc, 4, t_loc, CW), F32),
                vm((nc, 4, t_loc, CW), F32),
                vm((nc, 4, t_loc, CW), F32),
                dma((2 + d // KW,)), dma((NS, 2)),
                *[dma((d // KW, 4))] * 4, *[dma((4,))] * 8,
                dma((nc,)), dma((nc,)), dma((nc, 4)), dma((nc, 4)),
            ],
            compiler_params=pltpu.CompilerParams(collective_id=0, has_side_effects=True,
                                                 vmem_limit_bytes=67043328),
            name="moe",
        )(x, idx.T, g.T, w1.reshape(el, d // fl, fl, fl), w3.reshape(el, d // fl, fl, fl), w2)
        return y.astype(BF16)

    return jax.shard_map(local, mesh=mesh,
                         in_specs=(rows, rows, rows, P("ep", None, "tp"), P("ep", None, "tp"), P("ep", "tp", None)),
                         out_specs=rows, check_vma=False)
```

time: 50.3 us -> 51.6 us (1.026)
  Pallas kernels: 48.5 us -> 49.8 us
    pallas_call x1, Pallas kernels: 48.5 us -> 49.8 us  [local(): pl.pallas_call(functools.partial(_kernel, el, cap), out_shape=jax.ShapeDt...]
where the time goes in v3:
time: 51.6 us; the launch traced here: 51.5 us
  Pallas kernels  49.8 us (97%)
  other arithmetic  1.62 us (3%)
    pallas_call x1, Pallas kernels, local(): pl.pallas_call(functools.partial(_kernel, el, cap), out_shape=jax.ShapeDt...  49.8 us
    convert_element_type x1, other arithmetic, local(): return y.astype(BF16)  1.62 us

profile of v3, /device:TPU:0, one launch (start us, length us, event | category | flops | bytes accessed | tf_op | source)
XLA Modules:
  0.0 51.5 jit_solution(13496268655788391516)
XLA Ops:
  0.0 49.8 %moe.1 = f32[32,2048]{1,0:T(8,128)} custom-call(bf16[32,2048]{1,0:T(8,128)(2,1)} %x_ref.1, s32[8,32]{1,0:T(8,128)} %bitcast.6, f32[8,32]{1,0:T(8,128)} %bitcast.7, bf16[32,8,256,256]{3,2,1,0:T(8,128)(2,1)} %bitcast.4, bf16[32,8,256,256]{3,2,1,0:T(8,128)(2,1)} %bitcast.5, bf16[32,256,2048]{2,1,0:T(8,128)(2,1)} %w2_ref.1), custom_call_target="tpu_custom_call" | custom-call | tf_op jit(solution)/shard_map/moe/pallas_call | solution.py:332
  49.8 1.6 %convert_element_type.3 = bf16[32,2048]{1,0:T(8,128)(2,1)} convert(f32[32,2048]{1,0:T(8,128)} %moe.1) | non-fusion elementwise | flops 65536 | bytes 393216 | tf_op jit(solution)/shard_map/convert_element_type | solution.py:362

commit v4 on v0

v4 whole, which is shorter than its diff:
```python
import functools

import jax
import jax.numpy as jnp
from jax import lax
from jax.experimental import pallas as pl
from jax.experimental.pallas import tpu as pltpu
from jax.sharding import PartitionSpec as P

CF = 2
NP = 10
PRIME = (2, 6, NP)
KW = 512
NW = 8
UP = 8
CW = 256
F32, BF16 = jnp.float32, jnp.bfloat16


def _dot(a, b):
    return jnp.dot(a, b, preferred_element_type=F32)


def _kernel(n_el, cap, x_ref, idx_ref, g_ref, w1_ref, w3_ref, w2_ref, o_ref,
            xall, idxv, gv, sall, gall, xg, ring, acc, hbuf, gt, pt, ybuf, yacc, yrecv, ssum, rfin,
            in_sem, wsem, x_sem, xr_sem, xp_sem, s_sem, sr_sem, sp_sem, g_sem, gr_sem, gp_sem, y_sem, yr_sem, z_sem, zr_sem):
    ep, tp = lax.axis_index("ep"), lax.axis_index("tp")
    dp = lax.axis_index("dp")
    core = lax.rem(tp, 2)
    chip = ep * 2 + tp // 2
    t_loc, d = x_ref.shape
    top = idx_ref.shape[0]
    n_exp = 2 * n_el
    n_chunk = d // CW
    kd, fl = w1_ref.shape[2], w1_ref.shape[3]
    n_k = d // KW
    n_w13 = n_el // 2
    n_pair = n_w13 + n_chunk
    rows = pl.ds(core * t_loc, t_loc)
    other = pl.ds((1 - core) * t_loc, t_loc)

    def dev(r, flip):
        e2 = 1 - ep if r & 2 else ep
        x2 = 1 - tp // 2 if r & 1 else tp // 2
        c2 = 1 - core if flip else core
        return (dp, e2, x2 * 2 + c2)

    def chip_of(r):
        e2 = 1 - ep if r & 2 else ep
        x2 = 1 - tp // 2 if r & 1 else tp // 2
        return e2 * 2 + x2

    def remote(src, dst, ss, rs, to):
        return pltpu.make_async_remote_copy(src_ref=src, dst_ref=dst, send_sem=ss, recv_sem=rs, device_id=to,
                                            device_id_type=pl.DeviceIdType.MESH)

    def wait_bytes(ref, sem):
        pltpu.make_async_copy(ref, ref, sem).wait()

    def start(p):
        slot = lax.rem(p, NP)
        left, right = pl.ds(0, fl), pl.ds(fl, fl)

        @pl.when(p < n_w13)
        def _():
            for w, half in ((w1_ref, left), (w3_ref, right)):
                pltpu.make_async_copy(w.at[pl.ds(2 * p, 2)], ring.at[slot, :, :, :, half], wsem.at[slot]).start()

        @pl.when(jnp.logical_and(p >= n_w13, p < n_pair))
        def _():
            cols = pl.ds(pl.multiple_of((p - n_w13) * CW, CW), CW)
            for k, half in enumerate((left, right)):
                pltpu.make_async_copy(w2_ref.at[pl.ds(2 * k, 2), :, :, cols], ring.at[slot, :, :, :, half],
                                      wsem.at[slot]).start()

    def wait(p):
        slot = lax.rem(p, NP)
        wait_bytes(ring.at[slot], wsem.at[slot])

    def prime(p, _):
        start(p)
        return 0

    x_in = [pltpu.make_async_copy(x_ref.at[:, pl.ds(k * KW, KW)], xall.at[k, chip, rows], in_sem.at[2 + k])
            for k in range(n_k)]
    i_in = pltpu.make_async_copy(idx_ref, idxv, in_sem.at[0])
    g_in = pltpu.make_async_copy(g_ref, gv, in_sem.at[1])
    i_in.start()
    g_in.start()
    for c in x_in:
        c.start()
    barrier = pltpu.get_barrier_semaphore()
    peers = [(1, False), (2, False), (3, False), (0, True)]
    for r, flip in peers:
        pl.semaphore_signal(barrier, inc=1, device_id=dev(r, flip), device_id_type=pl.DeviceIdType.MESH)
    lax.fori_loop(0, PRIME[0], prime, 0)
    i_in.wait()
    g_in.wait()

    ids, gates = idxv[...], gv[...]
    line = lax.broadcasted_iota(jnp.int32, (2 * n_exp, t_loc), 0)
    gd = jnp.zeros((2 * n_exp, t_loc), F32)
    hit = jnp.zeros((2 * n_exp, t_loc), F32)
    for j in range(top):
        eq = ids[j:j + 1] == line
        gd = jnp.where(eq, gates[j:j + 1], gd)
        hit = jnp.where(eq, 1.0, hit)
    before = (lax.broadcasted_iota(jnp.int32, (t_loc, t_loc), 0)
              < lax.broadcasted_iota(jnp.int32, (t_loc, t_loc), 1)).astype(BF16)
    slot = _dot(hit.astype(BF16), before)
    keep = jnp.logical_and(hit > 0.5, slot < cap - 0.5)
    sall[chip, rows] = jnp.where(keep, slot, -1.0).T.astype(BF16)
    gall[chip, rows] = jnp.where(keep, gd, 0.0).T

    for c in x_in:
        c.wait()
    pl.semaphore_wait(barrier, len(peers))

    def block(buf, r, k, mine=True):
        at = buf if k is None else buf.at[k]
        return at.at[chip_of(r), rows if mine else other]

    def send(buf, ss, rs, ps, k, to=(3, 1, 2, 0)):
        for r in to:
            ref = block(buf, 0, k)
            remote(ref, ref, ss, rs.at[r] if r else ps.at[0], dev(r, r == 0)).start()

    def forward(buf, ss, rs, ps, k):
        for r in (2, 3, 1):
            ref = block(buf, r, k)
            remote(ref, ref, ss, rs.at[r], dev(r, False)).wait_recv()
            remote(ref, ref, ss, ps.at[r], dev(0, True)).start()

    def settle(buf, ss, ps, k, froms):
        for r in froms:
            ref = block(buf, r, k, False)
            remote(ref, ref, ss, ps.at[r], dev(0, True)).wait_recv()

    sg = (sall, s_sem.at[0], sr_sem, sp_sem, None)
    gg = (gall, g_sem.at[0], gr_sem, gp_sem, None)
    xs = [(xall, x_sem.at[0], xr_sem.at[k], xp_sem.at[k], k) for k in range(n_k)]
    send(*sg)
    for x in xs:
        send(*x)
    send(*gg)
    lax.fori_loop(PRIME[0], PRIME[1], prime, 0)

    pair = 2 * t_loc
    nk = n_el * 2 * cap
    m = 8 * cap
    el = lax.broadcasted_iota(jnp.int32, (2 * n_exp, nk), 1) // (2 * cap) + ep * n_el
    expand = (lax.broadcasted_iota(jnp.int32, (2 * n_exp, nk), 0) == el).astype(BF16)
    kl = lax.broadcasted_iota(jnp.int32, (pair, nk), 1)
    tr = lax.broadcasted_iota(jnp.int32, (pair, nk), 0)
    want = jnp.where(lax.rem(kl // cap, 2) == tr // t_loc, lax.rem(kl, cap), -2).astype(F32)

    def plan(r):
        q = chip_of(r)
        pt[q] = jnp.where(_dot(sall[q], expand) == want, 1.0, 0.0).T.astype(BF16)

    def dispatch(k, r):
        q = chip_of(r)
        got = _dot(pt[q], xall[k, q])
        xg[k, :, q] = got.astype(BF16).reshape(n_el, 2 * cap, KW)

    settle(sall, s_sem.at[0], sp_sem, None, (0,))
    for x in xs:
        settle(xall, x_sem.at[0], x[3], x[4], (0,))
    plan(0)
    for k in range(n_k):
        dispatch(k, 0)
    forward(*sg)
    settle(sall, s_sem.at[0], sp_sem, None, (2, 3, 1))
    for r in (2, 3, 1):
        plan(r)
    lax.fori_loop(PRIME[1], PRIME[2], prime, 0)

    def swiglu(v):
        a, b = v[:, :fl], v[:, fl:]
        return (a * jax.nn.sigmoid(a) * b).astype(BF16)

    forward(*xs[0])
    for k in range(n_k):
        settle(xall, x_sem.at[0], xs[k][3], k, (2, 3, 1))
        if k + 1 < n_k:
            forward(*xs[k + 1])
        else:
            forward(*gg)
        if k == 0:
            for p in range(NW // 2):
                wait(p)
        for r in (2, 3, 1):
            dispatch(k, r)
        nt = KW // kd
        for e in range(NW):
            w = ring[e // 2, e % 2, k * nt:(k + 1) * nt].reshape(KW, 2 * fl)
            v = _dot(xg[k, e].reshape(m, KW), w)
            v = v if k == 0 else acc[e] + v
            if k + 1 < n_k:
                acc[e] = v
            else:
                hbuf[e] = swiglu(v)
    for p in range(NW // 2):
        start(p + NP)

    settle(gall, g_sem.at[0], gp_sem, None, (0, 2, 3, 1))
    here = (_dot(sall[...].reshape(4 * pair, 2 * n_exp), expand).reshape(4, pair, nk) == want)
    gs = gall[...].reshape(4 * pair, 2 * n_exp)
    hi = gs.astype(BF16)
    r1 = gs - hi.astype(F32)
    mid = r1.astype(BF16)
    lo = (r1 - mid.astype(F32)).astype(BF16)
    for k, p in enumerate((hi, mid, lo)):
        gt[:, pl.ds(k * pair, pair)] = jnp.where(here, _dot(p, expand).reshape(4, pair, nk), 0.0).astype(BF16)

    def up(u, _):
        for j in range(UP // 2):
            wait(u * (UP // 2) + j)
        for j in range(UP):
            e = u * UP + j
            w = ring[lax.rem(u * (UP // 2) + j // 2, NP), j % 2].reshape(n_k, KW, 2 * fl)
            v = _dot(xg[0, e].reshape(m, KW), w[0])
            for k in range(1, n_k):
                v = v + _dot(xg[k, e].reshape(m, KW), w[k])
            hbuf[e] = swiglu(v)
        for j in range(UP // 2):
            start(u * (UP // 2) + j + NP)
        return 0

    lax.fori_loop(NW // UP, n_el // UP, up, 0)

    wait_bytes(xall.at[pl.ds(0, n_k - 1)], x_sem.at[0])
    wait_bytes(xall.at[0, pl.ds(0, n_k // 2)], x_sem.at[0])
    for buf, sem in ((sall, s_sem), (gall, g_sem)):
        wait_bytes(buf.at[pl.ds(0, 3)], sem.at[0])
        wait_bytes(buf.at[0, pl.ds(0, t_loc)], sem.at[0])

    def y_copy(c):
        return remote(yacc.at[c, 1 - core], yrecv.at[c], y_sem.at[0], yr_sem.at[c], dev(0, True))

    def second(c):
        y_copy(c).wait_recv()
        ssum[c] = yacc[c, core] + yrecv[c]
        for r in (3, 1, 2):
            remote(ssum.at[c, chip_of(r)], rfin.at[c, r - 1], z_sem.at[0], zr_sem.at[c], dev(r, False)).start()

    def products(c):
        for e in range(n_el):
            i, j = e // 8, e % 8
            w = ring[lax.rem(c + n_w13, NP), i % 2, j, :, (i // 2) * CW:(i // 2 + 1) * CW]
            ybuf[lax.rem(c, 2), e] = _dot(hbuf[e], w).astype(BF16).reshape(4, 2 * cap, CW)

    def combine(c):
        for p in range(4):
            z = _dot(gt[p], ybuf[lax.rem(c, 2), :, p].reshape(nk, CW))
            z = z[:pair] + z[pair:2 * pair] + z[2 * pair:]
            for k in range(2):
                yacc[c, k, p] = z[k * t_loc:(k + 1) * t_loc]

    wait(n_w13)
    products(0)

    def down(c, _):
        wait(n_w13 + c)
        combine(c - 1)
        products(c)
        y_copy(c - 1).start()

        @pl.when(c > 1)
        def _():
            second(c - 2)

        return 0

    lax.fori_loop(1, n_chunk, down, 0)
    combine(n_chunk - 1)
    second(n_chunk - 2)
    y_copy(n_chunk - 1).start()

    def total(c):
        wait_bytes(rfin.at[c], zr_sem.at[c])
        o_ref[:, pl.ds(pl.multiple_of(c * CW, CW), CW)] = ssum[c, chip] + rfin[c, 0] + rfin[c, 1] + rfin[c, 2]

    for c in range(n_chunk - 4):
        total(c)
    second(n_chunk - 1)
    for c in range(n_chunk - 4, n_chunk):
        total(c)
    wait_bytes(yrecv, y_sem.at[0])
    wait_bytes(rfin, z_sem.at[0])


def solution(mesh):
    rows = P(("dp", "ep", "tp"), None)

    def local(x, idx, g, w1, w3, w2):
        t_loc, d = x.shape
        top = idx.shape[1]
        el, _, fl = w1.shape
        n_exp = 2 * el
        cap = CF * top * t_loc // n_exp
        nc = d // CW
        nk = el * 2 * cap
        dma, vm = pltpu.SemaphoreType.DMA, pltpu.VMEM
        any_ = pl.BlockSpec(memory_space=pl.ANY)
        y = pl.pallas_call(
            functools.partial(_kernel, el, cap),
            out_shape=jax.ShapeDtypeStruct((t_loc, d), F32),
            in_specs=[any_] * 6,
            out_specs=pl.BlockSpec(memory_space=pltpu.VMEM),
            scratch_shapes=[
                vm((d // KW, 4, 2 * t_loc, KW), BF16),
                vm((top, t_loc), jnp.int32),
                vm((top, t_loc), F32),
                vm((4, 2 * t_loc, 2 * n_exp), BF16),
                vm((4, 2 * t_loc, 2 * n_exp), F32),
                vm((d // KW, el, 4, 2 * cap, KW), BF16),
                vm((NP, 2, d // fl, fl, 2 * fl), BF16),
                vm((NW, 8 * cap, 2 * fl), F32),
                vm((el, 8 * cap, fl), BF16),
                vm((4, 6 * t_loc, nk), BF16),
                vm((4, nk, 2 * t_loc), BF16),
                vm((2, el, 4, 2 * cap, CW), BF16),
                vm((nc, 2, 4, t_loc, CW), F32),
                vm((nc, 4, t_loc, CW), F32),
                vm((nc, 4, t_loc, CW), F32),
                vm((nc, 3, t_loc, CW), F32),
                dma((2 + d // KW,)), dma((NP,)),
                dma((1,)), dma((d // KW, 4)), dma((d // KW, 4)),
                dma((1,)), dma((4,)), dma((4,)),
                dma((1,)), dma((4,)), dma((4,)),
                dma((1,)), dma((nc,)), dma((1,)), dma((nc,)),
            ],
            compiler_params=pltpu.CompilerParams(collective_id=0, has_side_effects=True,
                                                 vmem_limit_bytes=67043328),
            name="moe",
        )(x, idx.T, g.T, w1.reshape(el, d // fl, fl, fl), w3.reshape(el, d // fl, fl, fl),
          w2.reshape(el // 8, 8, fl, d))
        return y.astype(BF16)

    return jax.shard_map(local, mesh=mesh,
                         in_specs=(rows, rows, rows, P("ep", None, "tp"), P("ep", None, "tp"), P("ep", "tp", None)),
                         out_specs=rows, check_vma=False)
```

time: 313 us -> 46.2 us (0.15)
  blocking collectives: 131 us -> 0 us
  waiting for transfers between devices: 80.4 us -> 0 us
  matrix products: 51.7 us -> 0 us
  Pallas kernels: 0 us -> 44.4 us
  local copies, waits for them, and re-layouts: 23.7 us -> 0 us
  between operations: 13.5 us -> 0.01 us
  other arithmetic: 8.7 us -> 1.62 us
  starting transfers between devices: 3.76 us -> 0 us
    all_to_all x2 -> x0, blocking collectives: 131 us -> none  [the longest x1 100 us: local(): parts = lax.all_to_all(yp, 'tp', 0, 0, tiled=True)]
    all_gather x1 -> x0, waiting for transfers between devices: 56 us -> none  [local(): allr = lax.all_gather(recv, 'tp', axis=0)]
    dot_general x3 -> x0, matrix products: 51.7 us -> none  [the longest x1 18.3 us: local(): h1 = jnp.einsum('erd,edf->erf', xe, w1, preferred_element_type=jnp.float32)]
    pallas_call x0 -> x1, Pallas kernels: none -> 44.4 us  [local(): pl.pallas_call(functools.partial(_kernel, el, cap), out_shape=jax.ShapeDt...]
    all_to_all x1 -> x0, waiting for transfers between devices: 24.3 us -> none  [local(): back = lax.all_to_all(y, 'ep', 0, 0, tiled=True).reshape(n_exp * cap, d)]
    reshape x1 -> x0, local copies, waits for them, and re-layouts: 8.26 us -> none  [local(): yp = yp.reshape(el, tp, ep, cap, d).transpose(1, 2, 0, 3, 4)]
    all_gather x1 -> x0, local copies, waits for them, and re-layouts: 8.25 us -> none  [local(): allr = lax.all_gather(recv, 'tp', axis=0)]
    reduce_sum x3 -> x0, other arithmetic: 7.32 us -> none  [the longest x1 5.59 us: local(): y = jnp.sum(parts.astype(jnp.float32), axis=0).astype(jnp.bfloat16)]
  transfers between devices with their start and end apart: 2 -> 0, of which waited for: 2 -> 0; matrix products, arithmetic and copies ran while one was open for 0% -> 0% of each run, Pallas kernels for 0% -> 0%
where the time goes in v4:
time: 46.2 us; the launch traced here: 46 us
  Pallas kernels  44.4 us (96%)
  other arithmetic  1.62 us (4%)
    pallas_call x1, Pallas kernels, local(): pl.pallas_call(functools.partial(_kernel, el, cap), out_shape=jax.ShapeDt...  44.4 us
    convert_element_type x1, other arithmetic, local(): return y.astype(BF16)  1.62 us

profile of v4, /device:TPU:0, one launch (start us, length us, event | category | flops | bytes accessed | tf_op | source)
XLA Modules:
  0.0 46.0 jit_solution(903208691190445733)
XLA Ops:
  0.0 44.4 %moe.1 = f32[32,2048]{1,0:T(8,128)} custom-call(bf16[32,2048]{1,0:T(8,128)(2,1)} %x_ref.1, s32[8,32]{1,0:T(8,128)} %bitcast.8, f32[8,32]{1,0:T(8,128)} %bitcast.9, bf16[32,8,256,256]{3,2,1,0:T(8,128)(2,1)} %bitcast.5, bf16[32,8,256,256]{3,2,1,0:T(8,128)(2,1)} %bitcast.6, bf16[4,8,256,2048]{3,2,1,0:T(8,128)(2,1)} %bitcast.7), custom_call_target="tpu_custom_call" | custom-call | tf_op jit(solution)/shard_map/moe/pallas_call | solution.py:306
  44.4 1.6 %convert_element_type.3 = bf16[32,2048]{1,0:T(8,128)(2,1)} convert(f32[32,2048]{1,0:T(8,128)} %moe.1) | non-fusion elementwise | flops 65536 | bytes 393216 | tf_op jit(solution)/shard_map/convert_element_type | solution.py:339

commit v5 on v4

--- a/solution.py
+++ b/solution.py
@@ -9,10 +9,10 @@
 
 CF = 2
 NP = 10
-PRIME = (2, 6, NP)
+PRIME = (3, 4, 5, 6)
 KW = 512
 NW = 8
-UP = 8
+UP = 4
 CW = 256
 F32, BF16 = jnp.float32, jnp.bfloat16
 
@@ -63,15 +63,22 @@
 
         @pl.when(p < n_w13)
         def _():
-            for w, half in ((w1_ref, left), (w3_ref, right)):
-                pltpu.make_async_copy(w.at[pl.ds(2 * p, 2)], ring.at[slot, :, :, :, half], wsem.at[slot]).start()
+            for i in range(2):
+                for w, half in ((w1_ref, left), (w3_ref, right)):
+                    for h in range(2):
+                        part = pl.ds(h * 4, 4)
+                        pltpu.make_async_copy(w.at[2 * p + i, part], ring.at[slot, i, part, :, half],
+                                              wsem.at[slot]).start()
 
         @pl.when(jnp.logical_and(p >= n_w13, p < n_pair))
         def _():
             cols = pl.ds(pl.multiple_of((p - n_w13) * CW, CW), CW)
-            for k, half in enumerate((left, right)):
-                pltpu.make_async_copy(w2_ref.at[pl.ds(2 * k, 2), :, :, cols], ring.at[slot, :, :, :, half],
-                                      wsem.at[slot]).start()
+            for i in range(2):
+                for k, half in enumerate((left, right)):
+                    for h in range(2):
+                        part = pl.ds(h * 4, 4)
+                        pltpu.make_async_copy(w2_ref.at[2 * k + i, part, :, cols], ring.at[slot, i, part, :, half],
+                                              wsem.at[slot]).start()
 
     def wait(p):
         slot = lax.rem(p, NP)
@@ -169,38 +176,48 @@
     plan(0)
     for k in range(n_k):
         dispatch(k, 0)
+    lax.fori_loop(PRIME[1], PRIME[2], prime, 0)
     forward(*sg)
     settle(sall, s_sem.at[0], sp_sem, None, (2, 3, 1))
     for r in (2, 3, 1):
         plan(r)
-    lax.fori_loop(PRIME[1], PRIME[2], prime, 0)
+    lax.fori_loop(PRIME[2], PRIME[3], prime, 0)
+
+    always = dp >= 0
+
+    def own(v, e):
+        return jnp.where(always, v[:m], v[m:]) if e % 2 == 0 else jnp.where(always, v[m:], v[:m])
 
     def swiglu(v):
         a, b = v[:, :fl], v[:, fl:]
         return (a * jax.nn.sigmoid(a) * b).astype(BF16)
 
     forward(*xs[0])
-    for k in range(n_k):
-        settle(xall, x_sem.at[0], xs[k][3], k, (2, 3, 1))
-        if k + 1 < n_k:
-            forward(*xs[k + 1])
-        else:
-            forward(*gg)
-        if k == 0:
-            for p in range(NW // 2):
-                wait(p)
+    for p in range(NW // 2):
+        wait(p)
+    acc[...] = jnp.zeros_like(acc)
+    nt = KW // kd
+
+    def stage(k, _):
+        settle(xall, x_sem.at[0], xp_sem.at[k], k, (2, 3, 1))
+
+        @pl.when(k + 1 < n_k)
+        def _():
+            forward(xall, x_sem.at[0], xr_sem.at[k + 1], xp_sem.at[k + 1], k + 1)
+
+        start(PRIME[3] + k)
         for r in (2, 3, 1):
             dispatch(k, r)
-        nt = KW // kd
         for e in range(NW):
-            w = ring[e // 2, e % 2, k * nt:(k + 1) * nt].reshape(KW, 2 * fl)
-            v = _dot(xg[k, e].reshape(m, KW), w)
-            v = v if k == 0 else acc[e] + v
-            if k + 1 < n_k:
-                acc[e] = v
-            else:
-                hbuf[e] = swiglu(v)
-    for p in range(NW // 2):
+            w = ring[e // 2, e % 2, pl.ds(k * nt, nt)].reshape(KW, 2 * fl)
+            acc[e] += own(_dot(xg[k, e // 2 * 2:e // 2 * 2 + 2].reshape(2 * m, KW), w), e)
+        return 0
+
+    lax.fori_loop(0, n_k, stage, 0)
+    forward(*gg)
+    for e in range(NW):
+        hbuf[e] = swiglu(acc[e])
+    for p in range(3):
         start(p + NP)
 
     settle(gall, g_sem.at[0], gp_sem, None, (0, 2, 3, 1))
@@ -214,17 +231,16 @@
         gt[:, pl.ds(k * pair, pair)] = jnp.where(here, _dot(p, expand).reshape(4, pair, nk), 0.0).astype(BF16)
 
     def up(u, _):
+        start(NP + 3 + u - NW // UP)
         for j in range(UP // 2):
             wait(u * (UP // 2) + j)
         for j in range(UP):
-            e = u * UP + j
             w = ring[lax.rem(u * (UP // 2) + j // 2, NP), j % 2].reshape(n_k, KW, 2 * fl)
-            v = _dot(xg[0, e].reshape(m, KW), w[0])
+            two = pl.ds(u * UP + j // 2 * 2, 2)
+            v = _dot(xg[0, two].reshape(2 * m, KW), w[0])
             for k in range(1, n_k):
-                v = v + _dot(xg[k, e].reshape(m, KW), w[k])
-            hbuf[e] = swiglu(v)
-        for j in range(UP // 2):
-            start(u * (UP // 2) + j + NP)
+                v = v + _dot(xg[k, two].reshape(2 * m, KW), w[k])
+            hbuf[u * UP + j] = swiglu(own(v, j))
         return 0
 
     lax.fori_loop(NW // UP, n_el // UP, up, 0)
@@ -248,7 +264,8 @@
         for e in range(n_el):
             i, j = e // 8, e % 8
             w = ring[lax.rem(c + n_w13, NP), i % 2, j, :, (i // 2) * CW:(i // 2 + 1) * CW]
-            ybuf[lax.rem(c, 2), e] = _dot(hbuf[e], w).astype(BF16).reshape(4, 2 * cap, CW)
+            y = own(_dot(hbuf[e // 2 * 2:e // 2 * 2 + 2].reshape(2 * m, fl), w), e)
+            ybuf[lax.rem(c, 2), e] = y.astype(BF16).reshape(4, 2 * cap, CW)
 
     def combine(c):
         for p in range(4):
@@ -257,14 +274,15 @@
             for k in range(2):
                 yacc[c, k, p] = z[k * t_loc:(k + 1) * t_loc]
 
-    wait(n_w13)
-    products(0)
-
     def down(c, _):
+        start(NP + 3 + n_el // UP - NW // UP + c)
         wait(n_w13 + c)
-        combine(c - 1)
+        combine(lax.rem(c + n_chunk - 1, n_chunk))
         products(c)
-        y_copy(c - 1).start()
+
+        @pl.when(c > 0)
+        def _():
+            y_copy(c - 1).start()
 
         @pl.when(c > 1)
         def _():
@@ -272,7 +290,7 @@
 
         return 0
 
-    lax.fori_loop(1, n_chunk, down, 0)
+    lax.fori_loop(0, n_chunk, down, 0)
     combine(n_chunk - 1)
     second(n_chunk - 2)
     y_copy(n_chunk - 1).start()

time: 46.2 us -> 44.8 us (0.970)
  Pallas kernels: 44.4 us -> 43 us
    pallas_call x1, Pallas kernels: 44.4 us -> 43 us  [local(): pl.pallas_call(functools.partial(_kernel, el, cap), out_shape=jax.ShapeDt...]
where the time goes in v5:
time: 44.8 us; the launch traced here: 44.6 us
  Pallas kernels  43 us (96%)
  other arithmetic  1.62 us (4%)
    pallas_call x1, Pallas kernels, local(): pl.pallas_call(functools.partial(_kernel, el, cap), out_shape=jax.ShapeDt...  43 us
    convert_element_type x1, other arithmetic, local(): return y.astype(BF16)  1.62 us

profile of v5, /device:TPU:0, one launch (start us, length us, event | category | flops | bytes accessed | tf_op | source)
XLA Modules:
  0.0 44.6 jit_solution(4962928965205384260)
XLA Ops:
  0.0 43.0 %moe.1 = f32[32,2048]{1,0:T(8,128)} custom-call(bf16[32,2048]{1,0:T(8,128)(2,1)} %x_ref.1, s32[8,32]{1,0:T(8,128)} %bitcast.8, f32[8,32]{1,0:T(8,128)} %bitcast.9, bf16[32,8,256,256]{3,2,1,0:T(8,128)(2,1)} %bitcast.5, bf16[32,8,256,256]{3,2,1,0:T(8,128)(2,1)} %bitcast.6, bf16[4,8,256,2048]{3,2,1,0:T(8,128)(2,1)} %bitcast.7), custom_call_target="tpu_custom_call" | custom-call | tf_op jit(solution)/shard_map/moe/pallas_call | solution.py:324
  43.0 1.6 %convert_element_type.3 = bf16[32,2048]{1,0:T(8,128)(2,1)} convert(f32[32,2048]{1,0:T(8,128)} %moe.1) | non-fusion elementwise | flops 65536 | bytes 393216 | tf_op jit(solution)/shard_map/convert_element_type | solution.py:357

commit v6 on v5

--- a/solution.py
+++ b/solution.py
@@ -9,7 +9,7 @@
 
 CF = 2
 NP = 10
-PRIME = (3, 4, 5, 6)
+PRIME = (4, 6, 8, NP)
 KW = 512
 NW = 8
 UP = 4
@@ -23,7 +23,7 @@
 
 def _kernel(n_el, cap, x_ref, idx_ref, g_ref, w1_ref, w3_ref, w2_ref, o_ref,
             xall, idxv, gv, sall, gall, xg, ring, acc, hbuf, gt, pt, ybuf, yacc, yrecv, ssum, rfin,
-            in_sem, wsem, x_sem, xr_sem, xp_sem, s_sem, sr_sem, sp_sem, g_sem, gr_sem, gp_sem, y_sem, yr_sem, z_sem, zr_sem):
+            in_sem, wsem, x_sem, xr_sem, xp_sem, s_sem, sr_sem, sp_sem, g_sem, gr_sem, gp_sem, y_sem, yr_sem, z_sem, zr_sem, obuf, o_sem):
     ep, tp = lax.axis_index("ep"), lax.axis_index("tp")
     dp = lax.axis_index("dp")
     core = lax.rem(tp, 2)
@@ -178,6 +178,7 @@
         dispatch(k, 0)
     lax.fori_loop(PRIME[1], PRIME[2], prime, 0)
     forward(*sg)
+    forward(*xs[0])
     settle(sall, s_sem.at[0], sp_sem, None, (2, 3, 1))
     for r in (2, 3, 1):
         plan(r)
@@ -192,7 +193,6 @@
         a, b = v[:, :fl], v[:, fl:]
         return (a * jax.nn.sigmoid(a) * b).astype(BF16)
 
-    forward(*xs[0])
     for p in range(NW // 2):
         wait(p)
     acc[...] = jnp.zeros_like(acc)
@@ -205,7 +205,6 @@
         def _():
             forward(xall, x_sem.at[0], xr_sem.at[k + 1], xp_sem.at[k + 1], k + 1)
 
-        start(PRIME[3] + k)
         for r in (2, 3, 1):
             dispatch(k, r)
         for e in range(NW):
@@ -217,7 +216,7 @@
     forward(*gg)
     for e in range(NW):
         hbuf[e] = swiglu(acc[e])
-    for p in range(3):
+    for p in range(NW // 2):
         start(p + NP)
 
     settle(gall, g_sem.at[0], gp_sem, None, (0, 2, 3, 1))
@@ -231,7 +230,6 @@
         gt[:, pl.ds(k * pair, pair)] = jnp.where(here, _dot(p, expand).reshape(4, pair, nk), 0.0).astype(BF16)
 
     def up(u, _):
-        start(NP + 3 + u - NW // UP)
         for j in range(UP // 2):
             wait(u * (UP // 2) + j)
         for j in range(UP):
@@ -241,6 +239,8 @@
             for k in range(1, n_k):
                 v = v + _dot(xg[k, two].reshape(2 * m, KW), w[k])
             hbuf[u * UP + j] = swiglu(own(v, j))
+        for j in range(UP // 2):
+            start(u * (UP // 2) + j + NP)
         return 0
 
     lax.fori_loop(NW // UP, n_el // UP, up, 0)
@@ -265,45 +265,47 @@
             i, j = e // 8, e % 8
             w = ring[lax.rem(c + n_w13, NP), i % 2, j, :, (i // 2) * CW:(i // 2 + 1) * CW]
             y = own(_dot(hbuf[e // 2 * 2:e // 2 * 2 + 2].reshape(2 * m, fl), w), e)
-            ybuf[lax.rem(c, 2), e] = y.astype(BF16).reshape(4, 2 * cap, CW)
+            ybuf[e] = y.astype(BF16).reshape(4, 2 * cap, CW)
 
     def combine(c):
         for p in range(4):
-            z = _dot(gt[p], ybuf[lax.rem(c, 2), :, p].reshape(nk, CW))
+            z = _dot(gt[p], ybuf[:, p].reshape(nk, CW))
             z = z[:pair] + z[pair:2 * pair] + z[2 * pair:]
             for k in range(2):
                 yacc[c, k, p] = z[k * t_loc:(k + 1) * t_loc]
 
     def down(c, _):
-        start(NP + 3 + n_el // UP - NW // UP + c)
         wait(n_w13 + c)
-        combine(lax.rem(c + n_chunk - 1, n_chunk))
         products(c)
+        combine(c)
+        y_copy(c).start()
 
         @pl.when(c > 0)
         def _():
-            y_copy(c - 1).start()
-
-        @pl.when(c > 1)
-        def _():
-            second(c - 2)
+            second(c - 1)
+
+        @pl.when(c > 4)
+        def _():
+            total(c - 5)
 
         return 0
 
-    lax.fori_loop(0, n_chunk, down, 0)
-    combine(n_chunk - 1)
-    second(n_chunk - 2)
-    y_copy(n_chunk - 1).start()
+    def o_copy(c):
+        cols = pl.ds(pl.multiple_of(c * CW, CW), CW)
+        return pltpu.make_async_copy(obuf.at[:, cols], o_ref.at[:, cols], o_sem.at[c])
 
     def total(c):
         wait_bytes(rfin.at[c], zr_sem.at[c])
-        o_ref[:, pl.ds(pl.multiple_of(c * CW, CW), CW)] = ssum[c, chip] + rfin[c, 0] + rfin[c, 1] + rfin[c, 2]
-
-    for c in range(n_chunk - 4):
+        cols = pl.ds(pl.multiple_of(c * CW, CW), CW)
+        obuf[:, cols] = ssum[c, chip] + rfin[c, 0] + rfin[c, 1] + rfin[c, 2]
+        o_copy(c).start()
+
+    lax.fori_loop(0, n_chunk, down, 0)
+    second(n_chunk - 1)
+    for c in range(n_chunk - 5, n_chunk):
         total(c)
-    second(n_chunk - 1)
-    for c in range(n_chunk - 4, n_chunk):
-        total(c)
+    for c in range(n_chunk):
+        o_copy(c).wait()
     wait_bytes(yrecv, y_sem.at[0])
     wait_bytes(rfin, z_sem.at[0])
 
@@ -325,7 +327,7 @@
             functools.partial(_kernel, el, cap),
             out_shape=jax.ShapeDtypeStruct((t_loc, d), F32),
             in_specs=[any_] * 6,
-            out_specs=pl.BlockSpec(memory_space=pltpu.VMEM),
+            out_specs=any_,
             scratch_shapes=[
                 vm((d // KW, 4, 2 * t_loc, KW), BF16),
                 vm((top, t_loc), jnp.int32),
@@ -338,7 +340,7 @@
                 vm((el, 8 * cap, fl), BF16),
                 vm((4, 6 * t_loc, nk), BF16),
                 vm((4, nk, 2 * t_loc), BF16),
-                vm((2, el, 4, 2 * cap, CW), BF16),
+                vm((el, 4, 2 * cap, CW), BF16),
                 vm((nc, 2, 4, t_loc, CW), F32),
                 vm((nc, 4, t_loc, CW), F32),
                 vm((nc, 4, t_loc, CW), F32),
@@ -348,6 +350,7 @@
                 dma((1,)), dma((4,)), dma((4,)),
                 dma((1,)), dma((4,)), dma((4,)),
                 dma((1,)), dma((nc,)), dma((1,)), dma((nc,)),
+                vm((t_loc, d), F32), dma((nc,)),
             ],
             compiler_params=pltpu.CompilerParams(collective_id=0, has_side_effects=True,
                                                  vmem_limit_bytes=67043328),

time: 44.8 us -> 43.4 us (0.969)
  Pallas kernels: 43 us -> 41.7 us
    pallas_call x1, Pallas kernels: 43 us -> 41.7 us  [local(): pl.pallas_call(functools.partial(_kernel, el, cap), out_shape=jax.ShapeDt...]
where the time goes in v6:
time: 43.4 us; the launch traced here: 43.3 us
  Pallas kernels  41.7 us (96%)
  other arithmetic  1.62 us (4%)
    pallas_call x1, Pallas kernels, local(): pl.pallas_call(functools.partial(_kernel, el, cap), out_shape=jax.ShapeDt...  41.7 us
    convert_element_type x1, other arithmetic, local(): return y.astype(BF16)  1.62 us

profile of v6, /device:TPU:0, one launch (start us, length us, event | category | flops | bytes accessed | tf_op | source)
XLA Modules:
  0.0 43.3 jit_solution(9144764167243543400)
XLA Ops:
  0.0 41.7 %moe.1 = f32[32,2048]{1,0:T(8,128)} custom-call(bf16[32,2048]{1,0:T(8,128)(2,1)} %x_ref.1, s32[8,32]{1,0:T(8,128)} %bitcast.8, f32[8,32]{1,0:T(8,128)} %bitcast.9, bf16[32,8,256,256]{3,2,1,0:T(8,128)(2,1)} %bitcast.5, bf16[32,8,256,256]{3,2,1,0:T(8,128)(2,1)} %bitcast.6, bf16[4,8,256,2048]{3,2,1,0:T(8,128)(2,1)} %bitcast.7), custom_call_target="tpu_custom_call" | custom-call | tf_op jit(solution)/shard_map/moe/pallas_call | solution.py:326
  41.7 1.6 %convert_element_type.3 = bf16[32,2048]{1,0:T(8,128)(2,1)} convert(f32[32,2048]{1,0:T(8,128)} %moe.1) | non-fusion elementwise | flops 65536 | bytes 393216 | tf_op jit(solution)/shard_map/convert_element_type | solution.py:360

commit v7 on v6

--- a/solution.py
+++ b/solution.py
@@ -8,7 +8,7 @@
 from jax.sharding import PartitionSpec as P
 
 CF = 2
-NP = 10
+NP = 11
 PRIME = (4, 6, 8, NP)
 KW = 512
 NW = 8
@@ -22,7 +22,7 @@
 
 
 def _kernel(n_el, cap, x_ref, idx_ref, g_ref, w1_ref, w3_ref, w2_ref, o_ref,
-            xall, idxv, gv, sall, gall, xg, ring, acc, hbuf, gt, pt, ybuf, yacc, yrecv, ssum, rfin,
+            xall, idxv, gv, sall, gall, xg, ring, acc, hbuf, gt, pt, ybuf, yacc, yrecv, rfin,
             in_sem, wsem, x_sem, xr_sem, xp_sem, s_sem, sr_sem, sp_sem, g_sem, gr_sem, gp_sem, y_sem, yr_sem, z_sem, zr_sem, obuf, o_sem):
     ep, tp = lax.axis_index("ep"), lax.axis_index("tp")
     dp = lax.axis_index("dp")
@@ -256,9 +256,9 @@
 
     def second(c):
         y_copy(c).wait_recv()
-        ssum[c] = yacc[c, core] + yrecv[c]
+        yacc[c, core] += yrecv[c]
         for r in (3, 1, 2):
-            remote(ssum.at[c, chip_of(r)], rfin.at[c, r - 1], z_sem.at[0], zr_sem.at[c], dev(r, False)).start()
+            remote(yacc.at[c, core, chip_of(r)], rfin.at[c, r - 1], z_sem.at[0], zr_sem.at[c], dev(r, False)).start()
 
     def products(c):
         for e in range(n_el):
@@ -297,7 +297,7 @@
     def total(c):
         wait_bytes(rfin.at[c], zr_sem.at[c])
         cols = pl.ds(pl.multiple_of(c * CW, CW), CW)
-        obuf[:, cols] = ssum[c, chip] + rfin[c, 0] + rfin[c, 1] + rfin[c, 2]
+        obuf[:, cols] = (yacc[c, core, chip] + rfin[c, 0] + rfin[c, 1] + rfin[c, 2]).astype(BF16)
         o_copy(c).start()
 
     lax.fori_loop(0, n_chunk, down, 0)
@@ -325,7 +325,7 @@
         any_ = pl.BlockSpec(memory_space=pl.ANY)
         y = pl.pallas_call(
             functools.partial(_kernel, el, cap),
-            out_shape=jax.ShapeDtypeStruct((t_loc, d), F32),
+            out_shape=jax.ShapeDtypeStruct((t_loc, d), BF16),
             in_specs=[any_] * 6,
             out_specs=any_,
             scratch_shapes=[
@@ -343,21 +343,20 @@
                 vm((el, 4, 2 * cap, CW), BF16),
                 vm((nc, 2, 4, t_loc, CW), F32),
                 vm((nc, 4, t_loc, CW), F32),
-                vm((nc, 4, t_loc, CW), F32),
                 vm((nc, 3, t_loc, CW), F32),
                 dma((2 + d // KW,)), dma((NP,)),
                 dma((1,)), dma((d // KW, 4)), dma((d // KW, 4)),
                 dma((1,)), dma((4,)), dma((4,)),
                 dma((1,)), dma((4,)), dma((4,)),
                 dma((1,)), dma((nc,)), dma((1,)), dma((nc,)),
-                vm((t_loc, d), F32), dma((nc,)),
+                vm((t_loc, d), BF16), dma((nc,)),
             ],
             compiler_params=pltpu.CompilerParams(collective_id=0, has_side_effects=True,
                                                  vmem_limit_bytes=67043328),
             name="moe",
         )(x, idx.T, g.T, w1.reshape(el, d // fl, fl, fl), w3.reshape(el, d // fl, fl, fl),
           w2.reshape(el // 8, 8, fl, d))
-        return y.astype(BF16)
+        return y
 
     return jax.shard_map(local, mesh=mesh,
                          in_specs=(rows, rows, rows, P("ep", None, "tp"), P("ep", None, "tp"), P("ep", "tp", None)),

time: 43.4 us -> 43.2 us (level)
  other arithmetic: 1.62 us -> 0 us
  local copies, waits for them, and re-layouts: 0 us -> 1.57 us
    convert_element_type x1 -> x0, other arithmetic: 1.62 us -> none  [local(): return y.astype(BF16)]
    unnamed x0 -> x1, local copies, waits for them, and re-layouts: none -> 1.57 us
where the time goes in v7:
time: 43.2 us; the launch traced here: 43 us
  Pallas kernels  41.5 us (96%)
  local copies, waits for them, and re-layouts  1.57 us (4%)
    pallas_call x1, Pallas kernels, local(): pl.pallas_call(functools.partial(_kernel, el, cap), out_shape=jax.ShapeDt...  41.5 us
    unnamed x1, local copies, waits for them, and re-layouts  1.57 us

profile of v7, /device:TPU:0, one launch (start us, length us, event | category | flops | bytes accessed | tf_op | source)
XLA Modules:
  0.0 43.0 jit_solution(2338787147464105865)
XLA Ops:
  0.0 41.5 %moe.1 = bf16[32,2048]{1,0:T(8,128)(2,1)} custom-call(bf16[32,2048]{1,0:T(8,128)(2,1)} %x_ref.1, s32[8,32]{1,0:T(8,128)} %bitcast.8, f32[8,32]{1,0:T(8,128)} %bitcast.9, bf16[32,8,256,256]{3,2,1,0:T(8,128)(2,1)} %bitcast.5, bf16[32,8,256,256]{3,2,1,0:T(8,128)(2,1)} %bitcast.6, bf16[4,8,256,2048]{3,2,1,0:T(8,128)(2,1)} %bitcast.7), custom_call_target="tpu_custom_call" | custom-call | tf_op jit(solution)/shard_map/moe/pallas_call | solution.py:326
  41.5 1.6 %copy.8 = bf16[32,2048]{1,0:T(8,128)(2,1)} copy(bf16[32,2048]{1,0:T(8,128)(2,1)} %moe.1) | data formatting | bytes 262144

commit v8 on v7

--- a/solution.py
+++ b/solution.py
@@ -8,12 +8,13 @@
 from jax.sharding import PartitionSpec as P
 
 CF = 2
-NP = 11
+NP = 10
 PRIME = (4, 6, 8, NP)
 KW = 512
 NW = 8
 UP = 4
 CW = 256
+NR = 5
 F32, BF16 = jnp.float32, jnp.bfloat16
 
 
@@ -23,7 +24,7 @@
 
 def _kernel(n_el, cap, x_ref, idx_ref, g_ref, w1_ref, w3_ref, w2_ref, o_ref,
             xall, idxv, gv, sall, gall, xg, ring, acc, hbuf, gt, pt, ybuf, yacc, yrecv, rfin,
-            in_sem, wsem, x_sem, xr_sem, xp_sem, s_sem, sr_sem, sp_sem, g_sem, gr_sem, gp_sem, y_sem, yr_sem, z_sem, zr_sem, obuf, o_sem):
+            in_sem, wsem, x_sem, xr_sem, xp_sem, s_sem, sr_sem, sp_sem, g_sem, gr_sem, gp_sem, y_sem, yr_sem, z_sem, zr_sem, obuf, o_sem, rmid, zm_sem):
     ep, tp = lax.axis_index("ep"), lax.axis_index("tp")
     dp = lax.axis_index("dp")
     core = lax.rem(tp, 2)
@@ -254,11 +255,31 @@
     def y_copy(c):
         return remote(yacc.at[c, 1 - core], yrecv.at[c], y_sem.at[0], yr_sem.at[c], dev(0, True))
 
+    halves = ((1, 2, pl.ds(0, CW // 2)), (2, 1, pl.ds(CW // 2, CW // 2)))
+
     def second(c):
         y_copy(c).wait_recv()
         yacc[c, core] += yrecv[c]
-        for r in (3, 1, 2):
-            remote(yacc.at[c, core, chip_of(r)], rfin.at[c, r - 1], z_sem.at[0], zr_sem.at[c], dev(r, False)).start()
+
+        @pl.when(c < NR)
+        def _():
+            for h, (r1, _, cols) in enumerate(halves):
+                for k, r in enumerate((3, r1)):
+                    remote(yacc.at[c, core, chip_of(r), :, cols], rmid.at[c, h, k], z_sem.at[0], zm_sem.at[c],
+                           dev(r1, False)).start()
+
+        @pl.when(c >= NR)
+        def _():
+            for r in (3, 1, 2):
+                remote(yacc.at[c, core, chip_of(r)], rfin.at[c, r - 1], z_sem.at[0], zr_sem.at[c], dev(r, False)).start()
+
+    def third(c):
+        wait_bytes(rmid.at[c], zm_sem.at[c])
+        for h, (_, r2, cols) in enumerate(halves):
+            yacc[c, core, chip_of(r2), :, cols] += rmid[c, h, 0]
+            yacc[c, core, chip, :, cols] += rmid[c, h, 1]
+            remote(yacc.at[c, core, chip_of(r2), :, cols], rfin.at[c, 0, :, cols], z_sem.at[0], zr_sem.at[c],
+                   dev(r2, False)).start()
 
     def products(c):
         for e in range(n_el):
@@ -284,9 +305,9 @@
         def _():
             second(c - 1)
 
-        @pl.when(c > 4)
-        def _():
-            total(c - 5)
+        @pl.when(jnp.logical_and(c > 2, c - 3 < NR))
+        def _():
+            third(c - 3)
 
         return 0
 
@@ -295,14 +316,20 @@
         return pltpu.make_async_copy(obuf.at[:, cols], o_ref.at[:, cols], o_sem.at[c])
 
     def total(c):
-        wait_bytes(rfin.at[c], zr_sem.at[c])
-        cols = pl.ds(pl.multiple_of(c * CW, CW), CW)
-        obuf[:, cols] = (yacc[c, core, chip] + rfin[c, 0] + rfin[c, 1] + rfin[c, 2]).astype(BF16)
+        cols = pl.ds(c * CW, CW)
+        if c < NR:
+            wait_bytes(rfin.at[c, 0], zr_sem.at[c])
+            obuf[:, cols] = (yacc[c, core, chip] + rfin[c, 0]).astype(BF16)
+        else:
+            wait_bytes(rfin.at[c], zr_sem.at[c])
+            obuf[:, cols] = (yacc[c, core, chip] + rfin[c, 0] + rfin[c, 1] + rfin[c, 2]).astype(BF16)
         o_copy(c).start()
 
     lax.fori_loop(0, n_chunk, down, 0)
+    for c in range(2):
+        total(c)
     second(n_chunk - 1)
-    for c in range(n_chunk - 5, n_chunk):
+    for c in range(2, n_chunk):
         total(c)
     for c in range(n_chunk):
         o_copy(c).wait()
@@ -350,6 +377,7 @@
                 dma((1,)), dma((4,)), dma((4,)),
                 dma((1,)), dma((nc,)), dma((1,)), dma((nc,)),
                 vm((t_loc, d), BF16), dma((nc,)),
+                vm((NR, 2, 2, t_loc, CW // 2), F32), dma((NR,)),
             ],
             compiler_params=pltpu.CompilerParams(collective_id=0, has_side_effects=True,
                                                  vmem_limit_bytes=67043328),

time: 43.2 us -> 43.6 us (level)
    pallas_call x1, Pallas kernels: 41.5 us -> 41.9 us  [local(): pl.pallas_call(functools.partial(_kernel, el, cap), out_shape=jax.ShapeDt...]
where the time goes in v8:
time: 43.6 us; the launch traced here: 43.5 us
  Pallas kernels  41.9 us (96%)
  local copies, waits for them, and re-layouts  1.57 us (4%)
    pallas_call x1, Pallas kernels, local(): pl.pallas_call(functools.partial(_kernel, el, cap), out_shape=jax.ShapeDt...  41.9 us
    unnamed x1, local copies, waits for them, and re-layouts  1.57 us

profile of v8, /device:TPU:0, one launch (start us, length us, event | category | flops | bytes accessed | tf_op | source)
XLA Modules:
  0.0 43.5 jit_solution(10652167026708248533)
XLA Ops:
  0.0 41.9 %moe.1 = bf16[32,2048]{1,0:T(8,128)(2,1)} custom-call(bf16[32,2048]{1,0:T(8,128)(2,1)} %x_ref.1, s32[8,32]{1,0:T(8,128)} %bitcast.8, f32[8,32]{1,0:T(8,128)} %bitcast.9, bf16[32,8,256,256]{3,2,1,0:T(8,128)(2,1)} %bitcast.5, bf16[32,8,256,256]{3,2,1,0:T(8,128)(2,1)} %bitcast.6, bf16[4,8,256,2048]{3,2,1,0:T(8,128)(2,1)} %bitcast.7), custom_call_target="tpu_custom_call" | custom-call | tf_op jit(solution)/shard_map/moe/pallas_call | solution.py:353
  41.9 1.6 %copy.8 = bf16[32,2048]{1,0:T(8,128)(2,1)} copy(bf16[32,2048]{1,0:T(8,128)(2,1)} %moe.1) | data formatting | bytes 262144
